TPU v7x, 256 devices: a whole 4x4x8 slice. The times are simulated.
256 devices in a mesh: group: 8 (over x, core), member: 32 (over z, y).
Axes of the slice: x: 4, y: 4, z: 8, core: 2. Of those that a mesh axis runs over, the one named last changes fastest.
Arguments:
- queries: bfloat16 [256, 32, 128], P(('group', 'member')), may hold values from -1.2 to 1.2
- pages: bfloat16 [1536, 1024, 128], P(('group', 'member')), may hold values from -1.2 to 1.2
- users: int32 [1536, 32], P(('group', 'member')), may hold values from 0 to 255, as said below
- page_count: int32 [1536], P(('group', 'member')), may hold values from 1 to 32
- teacher: float32 [1536, 32], P(('group', 'member')), may hold values from 4 to 12
Outputs:
- scores: float32 [1536, 32], P(('group', 'member'))
- query_grad: float32 [256, 32, 128], P(('group', 'member'))
- page_grad: bfloat16 [1536, 1024, 128], P(('group', 'member'))
Inputs may be any that keep to these rules, and one draw needn't show every extreme that they name: `users`: slots at or past page_count hold valid ids that are ignored. Queries are numbered in the order of their owning devices. Over the slots of the pages of one device, exactly 8 distinct queries of each group (of 32 consecutive query ids) appear, counting dead slots too.
All inputs are finite; a program needn't handle non-finite values.
Results may differ from a plain program's by a relative error of at most 0.014.
Values may be sent and summed in bfloat16 or wider, within the bound.
A program may use at most 64 MiB of HBM per device.

v0:
```python
import math

import jax
import jax.numpy as jnp
from jax import lax
from jax.sharding import Mesh
from jax.sharding import PartitionSpec as P

CAP = 8
GROUP_MEMBER = ("group_0", "group_1", "member_0", "member_1")
MEMBER = ("member_0", "member_1")
GROUP = ("group_0", "group_1")


normalized_exponent_divisor = 0.05


def sent_to_all(value, axis):
    copies = jnp.broadcast_to(value, (lax.axis_size(axis), *value.shape))
    return lax.all_to_all(copies, axis, split_axis=0, concat_axis=0, tiled=True)


def laid_out(parts, dim):
    shape = list(parts.shape[1:])
    shape[dim] *= parts.shape[0]
    return jnp.moveaxis(parts, 0, dim).reshape(shape)


def whole_of(value, axes, dim):
    far, near = axes
    initial = sent_to_all(value, far)
    parts = jnp.swapaxes(sent_to_all(initial, near), 0, 1)
    return laid_out(parts.reshape(-1, *value.shape), dim)


def side_by_side(arrays, axis, split_dim, concat_dim, along):
    widths = [math.prod(a.shape[along:]) for a in arrays]
    both = jnp.concatenate(
        [a.reshape(*a.shape[:along], w) for a, w in zip(arrays, widths)], axis=along
    )
    filled = lax.all_to_all(both, axis, split_axis=split_dim, concat_axis=concat_dim, tiled=True)
    parts = jnp.split(filled, [sum(widths[:k]) for k in range(1, len(widths))], axis=along)
    return tuple(
        (b.reshape(*filled.shape[:along], *a.shape[along:]) for a, b in zip(arrays, parts))
    )


def split_up(value, dim, peers):
    shape = value.shape
    parts = value.reshape(*shape[:dim], peers, shape[dim] // peers, *shape[dim + 1 :])
    return jnp.moveaxis(parts, dim, 0)


def summed_on_arrival(value, axis, dim):
    peers = lax.axis_size(axis)
    parts = lax.all_to_all(split_up(value, dim, peers), axis, 0, 0, tiled=True)
    return jnp.sum(parts.astype(jnp.float32), axis=0)


def body(queries, pages, users, page_count, teacher):
    gathered = whole_of(queries, (("group_0", "group_1", "member_0"), "member_1"), 0)
    slots = users.shape[1]
    tok_rows = queries.shape[1]
    width = queries.shape[2]
    features = tok_rows * width

    def page_step(unused, inputs):
        page_tile, user_row, active_total, teacher_row = inputs
        chosen = gathered[user_row].reshape(slots * tok_rows, width)
        cosine_affinity = lax.dot_general(
            chosen, page_tile, (((1,), (1,)), ((), ())), preferred_element_type=jnp.float32
        )
        pairing_coefficients = jax.nn.softmax(
            cosine_affinity / normalized_exponent_divisor, axis=-1
        )
        aligned_rating = jnp.sum(pairing_coefficients * cosine_affinity, axis=-1)
        score = jnp.sum(aligned_rating.reshape(slots, tok_rows), axis=-1)
        live = lax.iota(jnp.int32, slots) < active_total
        unaligned_rating = jnp.where(live, score - teacher_row, 0.0)
        mismatch_row_set = jnp.repeat(unaligned_rating, tok_rows)
        rating_gradient_factor = (
            mismatch_row_set[:, None]
            * pairing_coefficients
            * (1.0 + (cosine_affinity - aligned_rating[:, None]) / normalized_exponent_divisor)
        ).astype(jnp.bfloat16)
        query_part = jnp.dot(rating_gradient_factor, page_tile, preferred_element_type=jnp.float32)
        page_part = lax.dot_general(
            rating_gradient_factor,
            chosen,
            (((0,), (0,)), ((), ())),
            preferred_element_type=jnp.float32,
        )
        return (
            unused,
            (
                jnp.where(live, score, 0.0),
                query_part.reshape(slots, features),
                page_part.astype(jnp.bfloat16),
            ),
        )

    _, (scores, query_terms, page_grad) = lax.scan(
        page_step, jnp.int32(0), (pages, users, page_count, teacher)
    )
    flat_users = users.reshape(-1)
    stacked = query_terms.reshape(-1, features)
    group_rows = lax.axis_size(MEMBER) * queries.shape[0]
    num_groups = lax.axis_size(GROUP)
    query_ids = lax.iota(jnp.int32, num_groups * group_rows)
    slot_match = query_ids[:, None] == flat_users[None, :]
    used = jnp.any(slot_match, axis=1).reshape(num_groups, group_rows)
    rank = jnp.cumsum(used.astype(jnp.int32), axis=1) - 1
    slot_rank = jnp.sum(jnp.where(slot_match, rank.reshape(-1)[:, None], 0), axis=0)
    position = flat_users // group_rows * CAP + slot_rank
    placing = (lax.iota(jnp.int32, num_groups * CAP)[:, None] == position[None, :]).astype(
        jnp.float32
    )
    send_rows = jnp.dot(
        placing, stacked, precision=lax.Precision.HIGHEST, preferred_element_type=jnp.float32
    )
    send_rows = send_rows.reshape(num_groups, CAP, features)
    member_rows = lax.iota(jnp.int32, group_rows)
    hits = used[:, :, None] & (rank[:, :, None] == lax.iota(jnp.int32, CAP)[None, None, :])
    found = jnp.sum(jnp.where(hits, member_rows[None, :, None], 0), axis=1)
    send_ids = jnp.where(jnp.any(hits, axis=1), found, -1).astype(jnp.float32)
    recv_rows, recv_ids = tuple(
        (
            part.astype(jnp.float32)
            for part in side_by_side(
                (send_rows.astype(jnp.bfloat16), send_ids.astype(jnp.bfloat16)), GROUP, 0, 0, 2
            )
        )
    )
    landing = (member_rows.astype(jnp.float32)[:, None] == recv_ids.reshape(-1)[None, :]).astype(
        jnp.float32
    )
    table = jnp.dot(
        landing,
        recv_rows.reshape(-1, features),
        precision=lax.Precision.HIGHEST,
        preferred_element_type=jnp.float32,
    )
    own_rows = summed_on_arrival(table.astype(jnp.bfloat16), MEMBER, 0)
    query_grad = own_rows.reshape(queries.shape)
    return (scores, query_grad, page_grad)


def solution(mesh):
    torus = Mesh(mesh.devices.reshape(4, 2, 8, 4), ("group_0", "group_1", "member_0", "member_1"))
    in_specs = (
        P(GROUP_MEMBER, None, None),
        P(GROUP_MEMBER, None, None),
        P(GROUP_MEMBER, None),
        P(GROUP_MEMBER),
        P(GROUP_MEMBER, None),
    )
    out_specs = (P(GROUP_MEMBER, None), P(GROUP_MEMBER, None, None), P(GROUP_MEMBER, None, None))
    return jax.shard_map(body, mesh=torus, in_specs=in_specs, out_specs=out_specs, check_vma=False)
```

profile of v0, /device:TPU:1, one launch (start us, length us, event | category | flops | bytes accessed | tf_op | source)
XLA Modules:
  0.0 207.7 jit_solution(14581505102542467155)
XLA Ops:
  1.4 29.9 %all_to_all.23 = bf16[64,1,32,128]{3,2,1,0:T(8,128)(2,1)S(1)} all-to-all(bf16[64,1,32,128]{3,2,1,0:T(8,128)(2,1)S(1)} %broadcast_in_dim.77), channel_id=1, replica_groups=mesh['group_0'=4,'group_1'=2,'member_0'=8,'member_1'=4] {'group_0','grou..., dimensions={0} | all-to-all | bytes 1048576 | tf_op jit(solution)/shard_map/all_to_all | solution.py:20
  31.3 1.7 broadcast_in_dim.78
  32.9 4.2 %all-to-all-start.1 = ((bf16[4,64,1,32,128]{4,3,1,2,0:T(8,128)(2,1)}), bf16[4,64,1,32,128]{4,3,1,2,0:T(8,128)(2,1)S(1)}, u32[]{:S(2)}, u32[]{:S(2)}) async-start(bf16[4,64,1,32,128]{4,3,1,2,0:T(8,128)(2,1)} %broadcast_in_dim.78), calls=%async_computation.1 | async-start | bytes 4194304 | tf_op jit(solution)/shard_map/all_to_all | solution.py:20
  38.5 23.3 %all-to-all-done.1 = bf16[4,64,1,32,128]{4,3,1,2,0:T(8,128)(2,1)S(1)} async-done(((bf16[4,64,1,32,128]{4,3,1,2,0:T(8,128)(2,1)}), bf16[4,64,1,32,128]{4,3,1,2,0:T(8,128)(2,1)S(1)}, u32[]{:S(2)}, u32[]{:S(2)}) %all-to-all-start.1) | async-done | bytes 2097184 | tf_op jit(solution)/shard_map/all_to_all | solution.py:20
  61.8 2.0 copy.15
  63.9 104.6 %while.14 = (s32[]{:T(128)}, f32[6,32]{1,0:T(8,128)S(1)}, f32[6,32,4096]{2,1,0:T(8,128)}, bf16[6,1024,128]{2,1,0:T(8,128)(2,1)}, s32[6]{0:T(128)S(1)}, /*index=5...) while((s32[]{:T(128)}, f32[6,32]{1,0:T(8,128)S(1)}, ...), condition=%wide.region_5.6_spmd, body=%wide.region_0.5_spmd.sunk | while | flops 825359616 | bytes 44373836 | solution.py:102
  63.9 2.2 %gather_fusion = bf16[32,32,128]{2,1,0:T(8,128)(2,1)S(1)} fusion(bf16[256,32,128]{2,1,0:T(8,128)(2,1)} %get-tuple-element.164, s32[1024]{0:T(1024)S(1)} %pad_clamp_fusion.2), kind=kCustom, calls=%fused_computation.clone.1 | custom fusion | bytes 524416 | tf_op jit(solution)/shard_map/while/body/eval_jaxpr/gather | solution.py:69
  66.1 1.7 multiply_reduce_fusion.4
  73.6 3.6 %multiply_convert_fusion.2 = bf16[1024,1024]{0,1:T(8,128)(2,1)S(1)} fusion(f32[1024,1024]{0,1:T(8,128)} %copy-done, f32[1024]{0:T(1024)S(1)} %multiply_reduce_fusion.5, f32[1024]{0:T(1024)S(1)} %mul.43, f32[1024]{0:T(1024)S(1)} %fusion.47, f32[1024]{0:T(1024)S(1)} %get-tuple-element.133), kind=kLoop, calls=%fused_computation.1.clone.1 | loop fusion | flops 9437184 | bytes 6307840 | tf_op jit(solution)/shard_map/while/body/eval_jaxpr/convert_element_type | solution.py:85
  77.2 1.7 fusion.48
  81.3 2.2 %gather_fusion = bf16[32,32,128]{2,1,0:T(8,128)(2,1)S(1)} fusion(bf16[256,32,128]{2,1,0:T(8,128)(2,1)} %get-tuple-element.164, s32[1024]{0:T(1024)S(1)} %pad_clamp_fusion.2), kind=kCustom, calls=%fused_computation.clone.1 | custom fusion | bytes 524416 | tf_op jit(solution)/shard_map/while/body/eval_jaxpr/gather | solution.py:69
  83.5 1.7 multiply_reduce_fusion.4
  91.1 3.6 %multiply_convert_fusion.2 = bf16[1024,1024]{0,1:T(8,128)(2,1)S(1)} fusion(f32[1024,1024]{0,1:T(8,128)} %copy-done, f32[1024]{0:T(1024)S(1)} %multiply_reduce_fusion.5, f32[1024]{0:T(1024)S(1)} %mul.43, f32[1024]{0:T(1024)S(1)} %fusion.47, f32[1024]{0:T(1024)S(1)} %get-tuple-element.133), kind=kLoop, calls=%fused_computation.1.clone.1 | loop fusion | flops 9437184 | bytes 6307840 | tf_op jit(solution)/shard_map/while/body/eval_jaxpr/convert_element_type | solution.py:85
  94.7 1.7 fusion.48
  98.8 2.2 %gather_fusion = bf16[32,32,128]{2,1,0:T(8,128)(2,1)S(1)} fusion(bf16[256,32,128]{2,1,0:T(8,128)(2,1)} %get-tuple-element.164, s32[1024]{0:T(1024)S(1)} %pad_clamp_fusion.2), kind=kCustom, calls=%fused_computation.clone.1 | custom fusion | bytes 524416 | tf_op jit(solution)/shard_map/while/body/eval_jaxpr/gather | solution.py:69
  101.0 1.7 multiply_reduce_fusion.4
  108.5 3.6 %multiply_convert_fusion.2 = bf16[1024,1024]{0,1:T(8,128)(2,1)S(1)} fusion(f32[1024,1024]{0,1:T(8,128)} %copy-done, f32[1024]{0:T(1024)S(1)} %multiply_reduce_fusion.5, f32[1024]{0:T(1024)S(1)} %mul.43, f32[1024]{0:T(1024)S(1)} %fusion.47, f32[1024]{0:T(1024)S(1)} %get-tuple-element.133), kind=kLoop, calls=%fused_computation.1.clone.1 | loop fusion | flops 9437184 | bytes 6307840 | tf_op jit(solution)/shard_map/while/body/eval_jaxpr/convert_element_type | solution.py:85
  112.1 1.7 fusion.48
  116.2 2.2 %gather_fusion = bf16[32,32,128]{2,1,0:T(8,128)(2,1)S(1)} fusion(bf16[256,32,128]{2,1,0:T(8,128)(2,1)} %get-tuple-element.164, s32[1024]{0:T(1024)S(1)} %pad_clamp_fusion.2), kind=kCustom, calls=%fused_computation.clone.1 | custom fusion | bytes 524416 | tf_op jit(solution)/shard_map/while/body/eval_jaxpr/gather | solution.py:69
  125.9 3.6 %multiply_convert_fusion.2 = bf16[1024,1024]{0,1:T(8,128)(2,1)S(1)} fusion(f32[1024,1024]{0,1:T(8,128)} %copy-done, f32[1024]{0:T(1024)S(1)} %multiply_reduce_fusion.5, f32[1024]{0:T(1024)S(1)} %mul.43, f32[1024]{0:T(1024)S(1)} %fusion.47, f32[1024]{0:T(1024)S(1)} %get-tuple-element.133), kind=kLoop, calls=%fused_computation.1.clone.1 | loop fusion | flops 9437184 | bytes 6307840 | tf_op jit(solution)/shard_map/while/body/eval_jaxpr/convert_element_type | solution.py:85
  129.6 1.7 fusion.48
  133.6 2.2 %gather_fusion = bf16[32,32,128]{2,1,0:T(8,128)(2,1)S(1)} fusion(bf16[256,32,128]{2,1,0:T(8,128)(2,1)} %get-tuple-element.164, s32[1024]{0:T(1024)S(1)} %pad_clamp_fusion.2), kind=kCustom, calls=%fused_computation.clone.1 | custom fusion | bytes 524416 | tf_op jit(solution)/shard_map/while/body/eval_jaxpr/gather | solution.py:69
  135.8 1.7 multiply_reduce_fusion.4
  143.4 3.6 %multiply_convert_fusion.2 = bf16[1024,1024]{0,1:T(8,128)(2,1)S(1)} fusion(f32[1024,1024]{0,1:T(8,128)} %copy-done, f32[1024]{0:T(1024)S(1)} %multiply_reduce_fusion.5, f32[1024]{0:T(1024)S(1)} %mul.43, f32[1024]{0:T(1024)S(1)} %fusion.47, f32[1024]{0:T(1024)S(1)} %get-tuple-element.133), kind=kLoop, calls=%fused_computation.1.clone.1 | loop fusion | flops 9437184 | bytes 6307840 | tf_op jit(solution)/shard_map/while/body/eval_jaxpr/convert_element_type | solution.py:85
  147.0 1.7 fusion.48
  151.1 2.2 %gather_fusion = bf16[32,32,128]{2,1,0:T(8,128)(2,1)S(1)} fusion(bf16[256,32,128]{2,1,0:T(8,128)(2,1)} %get-tuple-element.164, s32[1024]{0:T(1024)S(1)} %pad_clamp_fusion.2), kind=kCustom, calls=%fused_computation.clone.1 | custom fusion | bytes 524416 | tf_op jit(solution)/shard_map/while/body/eval_jaxpr/gather | solution.py:69
  160.8 3.6 %multiply_convert_fusion.2 = bf16[1024,1024]{0,1:T(8,128)(2,1)S(1)} fusion(f32[1024,1024]{0,1:T(8,128)} %copy-done, f32[1024]{0:T(1024)S(1)} %multiply_reduce_fusion.5, f32[1024]{0:T(1024)S(1)} %mul.43, f32[1024]{0:T(1024)S(1)} %fusion.47, f32[1024]{0:T(1024)S(1)} %get-tuple-element.133), kind=kLoop, calls=%fused_computation.1.clone.1 | loop fusion | flops 9437184 | bytes 6307840 | tf_op jit(solution)/shard_map/while/body/eval_jaxpr/convert_element_type | solution.py:85
  164.4 1.7 fusion.48
  168.5 3.3 %convolution_convert_fusion.1 = bf16[8,8,4096]{2,1,0:T(8,128)(2,1)S(1)} fusion(f32[192,4096,1]{1,0,2:T(8,128)} %bitcast.79, s32[192]{0:T(256)S(1)} %multiply_add_fusion.1, s32[8,8]{1,0:T(8,128)S(1)} %multiply_add_fusion), kind=kOutput, calls=%fused_computation.29 | convolution fusion | flops 604254208 | bytes 3671040 | tf_op jit(solution)/shard_map/dot_general | solution.py:118
  172.6 6.6 %all-to-all-start.2 = ((bf16[8,8,4097]{2,1,0:T(8,128)(2,1)}), bf16[8,8,4097]{2,1,0:T(8,128)(2,1)S(1)}, u32[]{:S(2)}, u32[]{:S(2)}) async-start(bf16[8,8,4097]{2,1,0:T(8,128)(2,1)} %pad_maximum_fusion), calls=%async_computation.2 | async-start | bytes 1081344 | tf_op jit(solution)/shard_map/all_to_all | solution.py:41
  179.3 9.5 %all-to-all-done.2 = bf16[8,8,4097]{2,1,0:T(8,128)(2,1)S(1)} async-done(((bf16[8,8,4097]{2,1,0:T(8,128)(2,1)}), bf16[8,8,4097]{2,1,0:T(8,128)(2,1)S(1)}, u32[]{:S(2)}, u32[]{:S(2)}) %all-to-all-start.2) | async-done | bytes 524448 | tf_op jit(solution)/shard_map/all_to_all | solution.py:41
  190.7 15.6 %all_to_all.24 = bf16[32,2,2048]{2,1,0:T(2,128)(2,1)S(1)} all-to-all(bf16[32,2,2048]{2,1,0:T(2,128)(2,1)S(1)} %reshape.197), channel_id=1, replica_groups=mesh['group_0'=4,'group_1'=2,'member_0'=8,'member_1'=4] {'member_0','mem..., dimensions={0} | all-to-all | bytes 524288 | tf_op jit(solution)/shard_map/all_to_all | solution.py:56
  (138 shorter events, 58.9 us)
Async XLA Ops:
  31.3 5.9 %copy-start.1 = (s32[6,32]{1,0:T(8,128)S(1)}, s32[6,32]{1,0:T(8,128)}, u32[]{:S(2)}) copy-start(s32[6,32]{1,0:T(8,128)} %param.9) | copy-start | bytes 2308
  32.9 28.9 %all-to-all-start.1 = ((bf16[4,64,1,32,128]{4,3,1,2,0:T(8,128)(2,1)}), bf16[4,64,1,32,128]{4,3,1,2,0:T(8,128)(2,1)S(1)}, u32[]{:S(2)}, u32[]{:S(2)}) async-start(bf16[4,64,1,32,128]{4,3,1,2,0:T(8,128)(2,1)} %broadcast_in_dim.78), calls=%async_computation.1 | async-start | bytes 4194304 | tf_op jit(solution)/shard_map/all_to_all | solution.py:20
  37.1 26.7 %copy-start.3 = (s32[6]{0:T(128)S(1)}, s32[6]{0:T(128)}, u32[]{:S(2)}) copy-start(s32[6]{0:T(128)} %param.10) | copy-start | bytes 76
  67.8 1.9 copy-start
  85.2 1.9 copy-start
  102.6 1.9 copy-start
  120.1 1.9 copy-start
  137.5 1.9 copy-start
  155.0 1.9 copy-start
  168.5 20.7 %copy-start.2 = (f32[6,32]{1,0:T(8,128)}, f32[6,32]{1,0:T(8,128)S(1)}, u32[]{:S(2)}) copy-start(f32[6,32]{1,0:T(8,128)S(1)} %get-tuple-element.49) | copy-start | bytes 2308
  172.6 16.2 %all-to-all-start.2 = ((bf16[8,8,4097]{2,1,0:T(8,128)(2,1)}), bf16[8,8,4097]{2,1,0:T(8,128)(2,1)S(1)}, u32[]{:S(2)}, u32[]{:S(2)}) async-start(bf16[8,8,4097]{2,1,0:T(8,128)(2,1)} %pad_maximum_fusion), calls=%async_computation.2 | async-start | bytes 1081344 | tf_op jit(solution)/shard_map/all_to_all | solution.py:41
where the time goes:
time: 210 us; the launch traced here: 208 us
  other arithmetic  48.4 us (23%)
  blocking collectives  45.4 us (22%)
  local copies, waits for them, and re-layouts  37 us (18%)
  waiting for transfers between devices  32.8 us (16%)
  matrix products  32.2 us (15%)
  starting transfers between devices  10.8 us (5%)
    all_to_all x1, blocking collectives, sent_to_all(): return lax.all_to_all(copies, axis, split_axis=0, concat_axis=0, tiled=True)  29.9 us
    all_to_all x1, waiting for transfers between devices, sent_to_all(): return lax.all_to_all(copies, axis, split_axis=0, concat_axis=0, tiled=True)  23.3 us
    convert_element_type x6, other arithmetic, page_step(): rating_gradient_factor = (mismatch_row_set[:, None] * pairing_coefficient...  21.7 us
    all_to_all x1, blocking collectives, summed_on_arrival(): parts = lax.all_to_all(split_up(value, dim, peers), axis, 0, 0, tiled=True)  15.6 us
    gather x6, local copies, waits for them, and re-layouts, page_step(): chosen = gathered[user_row].reshape(slots * tok_rows, width)  13.2 us
    dot_general x6, matrix products, page_step(): jnp.dot(rating_gradient_factor, page_tile, preferred_element_type=jnp.flo...  10.1 us
    dot_general x6, matrix products, page_step(): lax.dot_general(chosen, page_tile, (((1,), (1,)), ((), ())), preferred_el...  10 us
    all_to_all x1, waiting for transfers between devices, side_by_side(): lax.all_to_all(both, axis, split_axis=split_dim, concat_axis=concat_dim,...  9.52 us
  transfers between devices with their start and end apart: 2, of which 2 were waited for; matrix products, arithmetic and copies ran while one was open for 1% of the time, Pallas kernels for 0%

commit v1 on v0

v1 whole, which is shorter than its diff:
```python
import functools
import math

import jax
import jax.numpy as jnp
from jax import lax
from jax.experimental import pallas as pl
from jax.experimental.pallas import tpu as pltpu
from jax.sharding import PartitionSpec as P

MESH = pl.DeviceIdType.MESH
CAP = 8
GROUPS = 8
MEMBERS = 32
TOK = 32
DIM = 128
CHUNK = 8
LANES = CHUNK * TOK
INV_AT = 32
SCALE = math.log2(math.e) / 0.05
LN2 = math.log(2.0)


def greet(me_g, me_m):
    barrier = pltpu.get_barrier_semaphore()

    def to_member(k, carry):
        pl.semaphore_signal(
            barrier, inc=1, device_id=(me_g, (me_m + k) % MEMBERS), device_id_type=MESH
        )
        return carry

    lax.fori_loop(1, MEMBERS, to_member, 0)
    for k in range(1, GROUPS):
        pl.semaphore_signal(
            barrier, inc=1, device_id=((me_g + k) % GROUPS, me_m), device_id_type=MESH
        )
    return barrier


def fetch_kernel(
    query_ref, users_ref, picked_ref, lut_ref, info_ref,
    table, asks_out, asks_in, asks_smem, chosen,
    q_send, q_recv, a_send, a_recv, c_send, c_recv, local_sem,
):
    me_g = lax.axis_index("group")
    me_m = lax.axis_index("member")
    barrier = greet(me_g, me_m)

    total = GROUPS * MEMBERS
    rows = users_ref.shape[0]
    qid = lax.broadcasted_iota(jnp.int32, (total, users_ref.shape[1]), 0)
    hit = jnp.zeros(qid.shape, jnp.float32)
    for p in range(rows):
        hit = jnp.where(users_ref[p : p + 1, :] == qid, 1.0, hit)
    count = lax.dot_general(
        jnp.ones((8, users_ref.shape[1]), jnp.bfloat16),
        hit.astype(jnp.bfloat16),
        (((1,), (1,)), ((), ())),
        preferred_element_type=jnp.float32,
    )
    used = jnp.where(count > 0.5, 1.0, 0.0)
    ri = lax.broadcasted_iota(jnp.int32, (total, total), 0)
    ci = lax.broadcasted_iota(jnp.int32, (total, total), 1)
    before = jnp.where((ri < ci) & ((ri >> 5) == (ci >> 5)), 1.0, 0.0).astype(jnp.bfloat16)
    rank = jnp.dot(used.astype(jnp.bfloat16), before, preferred_element_type=jnp.float32)
    lane8 = lax.broadcasted_iota(jnp.int32, (8, total), 1)
    sub8 = lax.broadcasted_iota(jnp.int32, (8, total), 0)
    lut_ref[...] = (lane8 >> 5) * CAP + rank.astype(jnp.int32)
    of_group = (lane8 >> 5) == sub8
    k_id = lax.broadcasted_iota(jnp.int32, (128, total), 0).astype(jnp.float32)
    local_id = (lax.broadcasted_iota(jnp.int32, (128, total), 1) & 31).astype(jnp.float32)
    named = jnp.where((k_id == rank[0:1]) & (used[0:1] > 0.5), local_id, 0.0)
    ids = lax.dot_general(
        jnp.where(of_group, 1.0, 0.0).astype(jnp.bfloat16),
        named.astype(jnp.bfloat16),
        (((1,), (1,)), ((), ())),
        preferred_element_type=jnp.float32,
    )
    inverse = jnp.where(of_group, jnp.where(used > 0.5, rank, float(CAP)), 0.0)
    fold_r = lax.broadcasted_iota(jnp.int32, (total, 128), 0)
    fold_c = lax.broadcasted_iota(jnp.int32, (total, 128), 1)
    fold = jnp.where(fold_c == INV_AT + (fold_r & 31), 1.0, 0.0).astype(jnp.bfloat16)
    spread = jnp.dot(inverse.astype(jnp.bfloat16), fold, preferred_element_type=jnp.float32)
    asks = (ids + spread).astype(jnp.int32)
    for g in range(GROUPS):
        asks_out[g] = asks[g : g + 1, :]

    pl.semaphore_wait(barrier, MEMBERS - 1 + GROUPS - 1)

    def query_copy(k, src_m):
        peer = (me_m + k) % MEMBERS
        return pltpu.make_async_remote_copy(
            src_ref=query_ref.at[0],
            dst_ref=table.at[src_m],
            send_sem=q_send.at[k],
            recv_sem=q_recv.at[src_m],
            device_id=(me_g, peer),
            device_id_type=MESH,
        )

    def ask_copy(k, src_g):
        peer = (me_g + k) % GROUPS
        return pltpu.make_async_remote_copy(
            src_ref=asks_out.at[peer],
            dst_ref=asks_in.at[src_g],
            send_sem=a_send.at[k],
            recv_sem=a_recv.at[src_g],
            device_id=(peer, me_m),
            device_id_type=MESH,
        )

    def chosen_copy(k, src_g):
        peer = (me_g + k) % GROUPS
        return pltpu.make_async_remote_copy(
            src_ref=chosen.at[k],
            dst_ref=picked_ref.at[pl.ds(src_g * CAP, CAP)],
            send_sem=c_send.at[k],
            recv_sem=c_recv.at[src_g],
            device_id=(peer, me_m),
            device_id_type=MESH,
        )

    for k in range(1, GROUPS):
        ask_copy(k, me_g).start()

    def send_query(k, carry):
        query_copy(k, me_m).start()
        return carry

    lax.fori_loop(1, MEMBERS, send_query, 0)
    table[me_m] = query_ref[0]
    asks_in[me_g] = asks_out[me_g]
    for k in range(1, GROUPS):
        ask_copy(k, (me_g + k) % GROUPS).wait_recv()
    to_smem = pltpu.make_async_copy(asks_in, asks_smem, local_sem)
    to_smem.start()
    info_ref[...] = asks_in[...]
    to_smem.wait()

    def got_query(k, carry):
        query_copy(k, (me_m + k) % MEMBERS).wait_recv()
        return carry

    lax.fori_loop(1, MEMBERS, got_query, 0)
    for k in (4, 5, 2, 3, 6, 7, 1):
        peer = (me_g + k) % GROUPS
        for n in range(CAP):
            chosen[k, n] = table[asks_smem[peer, 0, n] & (MEMBERS - 1)]
        chosen_copy(k, me_g).start()
    for n in range(CAP):
        picked_ref[me_g * CAP + n] = table[asks_smem[me_g, 0, n] & (MEMBERS - 1)]
    for k in range(1, GROUPS):
        chosen_copy(k, (me_g + k) % GROUPS).wait_recv()
    for k in range(1, GROUPS):
        ask_copy(k, me_g).wait_send()
        chosen_copy(k, me_g).wait_send()

    def sent_query(k, carry):
        query_copy(k, me_m).wait_send()
        return carry

    lax.fori_loop(1, MEMBERS, sent_query, 0)


def fetch(queries, users):
    return pl.pallas_call(
        fetch_kernel,
        out_shape=(
            jax.ShapeDtypeStruct((GROUPS * CAP, TOK, DIM), jnp.bfloat16),
            jax.ShapeDtypeStruct((8, GROUPS * MEMBERS), jnp.int32),
            jax.ShapeDtypeStruct((GROUPS, 1, 128), jnp.int32),
        ),
        in_specs=[pl.BlockSpec(memory_space=pltpu.VMEM)] * 2,
        out_specs=[pl.BlockSpec(memory_space=pltpu.VMEM)] * 3,
        scratch_shapes=[
            pltpu.VMEM((MEMBERS, TOK, DIM), jnp.bfloat16),
            pltpu.VMEM((GROUPS, 1, 128), jnp.int32),
            pltpu.VMEM((GROUPS, 1, 128), jnp.int32),
            pltpu.SMEM((GROUPS, 1, 128), jnp.int32),
            pltpu.VMEM((GROUPS, CAP, TOK, DIM), jnp.bfloat16),
            pltpu.SemaphoreType.DMA((MEMBERS,)),
            pltpu.SemaphoreType.DMA((MEMBERS,)),
            pltpu.SemaphoreType.DMA((GROUPS,)),
            pltpu.SemaphoreType.DMA((GROUPS,)),
            pltpu.SemaphoreType.DMA((GROUPS,)),
            pltpu.SemaphoreType.DMA((GROUPS,)),
            pltpu.SemaphoreType.DMA,
        ],
        compiler_params=pltpu.CompilerParams(collective_id=0, has_side_effects=True),
        name="fetch",
    )(queries, users)


def split_dot(value, ones):
    high = value.astype(jnp.bfloat16)
    rest = value - high.astype(jnp.float32)
    mid = rest.astype(jnp.bfloat16)
    low = (rest - mid.astype(jnp.float32)).astype(jnp.bfloat16)
    dot = functools.partial(jnp.dot, preferred_element_type=jnp.float32)
    return dot(high, ones) + (dot(mid, ones) + dot(low, ones))


def match_kernel(
    users_ref, lut_ref, count_ref, teacher_ref, picked_ref, pages_ref,
    scores_ref, rows_ref, grad_ref,
    chunks, page_t, sims, logit, expo, stats, acc, row_acc, score_l, same_slot,
):
    n_pages, n_tok, _ = pages_ref.shape
    per_page = users_ref.shape[1] // CHUNK
    blocks = n_tok // 256

    def list_chunk(n, total):
        p = n // per_page
        alive = (n % per_page) * CHUNK < count_ref[p]

        @pl.when(alive)
        def _():
            chunks[total] = n

        return total + alive.astype(jnp.int32)

    total = lax.fori_loop(0, n_pages * per_page, list_chunk, 0)
    chunks[total] = chunks[total - 1]
    for p in range(n_pages):
        page_t[p] = pages_ref[p].T
    acc[...] = jnp.zeros_like(acc)
    row_acc[...] = jnp.zeros_like(row_acc)
    score_l[...] = jnp.zeros_like(score_l)
    seg_r = lax.broadcasted_iota(jnp.int32, (LANES, LANES), 0) >> 5
    seg_c = lax.broadcasted_iota(jnp.int32, (LANES, LANES), 1) >> 5
    same_slot[...] = jnp.where(seg_r == seg_c, 1.0, 0.0).astype(jnp.bfloat16)
    slot_of_lane = lax.broadcasted_iota(jnp.int32, (8, LANES), 1) >> 5

    def where_of(n):
        code = chunks[n]
        return code // per_page, code % per_page

    def picked_at(p, c, k):
        return lut_ref[0, users_ref[p, c * CHUNK + k]]

    def chosen_of(p, c):
        return jnp.concatenate(
            [picked_ref[picked_at(p, c, k)] for k in range(CHUNK)], axis=0
        )

    def fold8(value, op):
        parts = [value[8 * i : 8 * i + 8] for i in range(value.shape[0] // 8)]
        while len(parts) > 1:
            parts = [
                op(parts[i], parts[i + 1]) if i + 1 < len(parts) else parts[i]
                for i in range(0, len(parts), 2)
            ]
        return parts[0]

    def similar_of(n):
        p, c = where_of(n)
        chosen = chosen_of(p, c)
        top = None
        for b in range(blocks):
            block = lax.dot_general(
                pages_ref[p, 256 * b : 256 * b + 256, :],
                chosen,
                (((1,), (1,)), ((), ())),
                preferred_element_type=jnp.float32,
            )
            sims[256 * b : 256 * b + 256, :] = block
            high = fold8(block, jnp.maximum)
            top = high if top is None else jnp.maximum(top, high)
        return jnp.broadcast_to(jnp.max(top, axis=0, keepdims=True), (8, LANES))

    def weigh(top):
        mass = jnp.zeros((8, LANES), jnp.float32)
        moment = jnp.zeros((8, LANES), jnp.float32)
        top64 = jnp.concatenate([top] * 8, axis=0)
        for b in range(n_tok // 64):
            at = slice(64 * b, 64 * b + 64)
            t = (sims[at, :] - top64) * SCALE
            e = jnp.exp2(t)
            mass += fold8(e, jnp.add)
            moment += fold8(e * t, jnp.add)
            logit[at, :] = t
            expo[at, :] = e
        return mass, moment

    def finish(n, top, mass, moment):
        p, c = where_of(n)
        mass = jnp.broadcast_to(jnp.sum(mass, axis=0, keepdims=True), (8, LANES))
        moment = jnp.broadcast_to(jnp.sum(moment, axis=0, keepdims=True), (8, LANES))
        mean = moment / mass
        matched = top + mean * (1.0 / SCALE)
        score = split_dot(matched, same_slot[...])
        taught = jnp.zeros((8, LANES), jnp.float32)
        for k in range(CHUNK):
            taught = jnp.where(slot_of_lane == k, teacher_ref[p, c * CHUNK + k], taught)
        live = slot_of_lane + c * CHUNK < count_ref[p]
        score_l[c, pl.ds(p, 1), :] = jnp.where(live, score, 0.0)[0:1]
        part = jnp.where(live, score - taught, 0.0) / mass
        slant = part * LN2
        base = part - slant * mean
        chosen = chosen_of(p, c)
        base64 = jnp.concatenate([base] * 8, axis=0)
        slant64 = jnp.concatenate([slant] * 8, axis=0)
        query_t = jnp.zeros((DIM, LANES), jnp.float32)
        for b in range(blocks):
            parts = []
            for i in range(4):
                at = slice(256 * b + 64 * i, 256 * b + 64 * i + 64)
                parts.append(
                    (expo[at, :] * (base64 + slant64 * logit[at, :])).astype(jnp.bfloat16)
                )
            slope = jnp.concatenate(parts, axis=0)
            at = slice(256 * b, 256 * b + 256)
            acc[p, at, :] += jnp.dot(slope, chosen, preferred_element_type=jnp.float32)
            query_t += jnp.dot(page_t[p, :, at], slope, preferred_element_type=jnp.float32)
        query_part = query_t.T
        for k in range(CHUNK):
            row_acc[picked_at(p, c, k)] += query_part[TOK * k : TOK * k + TOK]

    def step(n, carry):
        top = similar_of(n)
        mass, moment = weigh(top)
        finish(n, top, mass, moment)
        return carry

    lax.fori_loop(0, total, step, 0)

    col = lax.broadcasted_iota(jnp.int32, (LANES, 128), 1)
    row = lax.broadcasted_iota(jnp.int32, (LANES, 128), 0)
    out = jnp.zeros((8, 128), jnp.float32)
    for c in range(per_page):
        take = jnp.where(row == (col - c * CHUNK) * TOK, 1.0, 0.0)
        out += split_dot(score_l[c], take.astype(jnp.bfloat16))
    scores_ref[...] = out[: scores_ref.shape[0], : scores_ref.shape[1]]
    for p in range(n_pages):
        grad_ref[p] = acc[p].astype(jnp.bfloat16)
    rows_ref[...] = row_acc[...].astype(jnp.bfloat16)


def match(users, lut, page_count, teacher, picked, pages):
    n_pages, n_tok, _ = pages.shape
    per_page = users.shape[1] // CHUNK
    smem = pl.BlockSpec(memory_space=pltpu.SMEM)
    vmem = pl.BlockSpec(memory_space=pltpu.VMEM)
    return pl.pallas_call(
        match_kernel,
        out_shape=(
            jax.ShapeDtypeStruct(users.shape, jnp.float32),
            jax.ShapeDtypeStruct(picked.shape, jnp.bfloat16),
            jax.ShapeDtypeStruct(pages.shape, jnp.bfloat16),
        ),
        in_specs=[smem, smem, smem, smem, vmem, vmem],
        out_specs=[vmem, vmem, vmem],
        scratch_shapes=[
            pltpu.SMEM((n_pages * per_page + 1,), jnp.int32),
            pltpu.VMEM((n_pages, DIM, n_tok), jnp.bfloat16),
            pltpu.VMEM((n_tok, LANES), jnp.float32),
            pltpu.VMEM((n_tok, LANES), jnp.float32),
            pltpu.VMEM((n_tok, LANES), jnp.float32),
            pltpu.VMEM((8, LANES), jnp.float32),
            pltpu.VMEM((n_pages, n_tok, DIM), jnp.float32),
            pltpu.VMEM(picked.shape, jnp.float32),
            pltpu.VMEM((per_page, 8, LANES), jnp.float32),
            pltpu.VMEM((LANES, LANES), jnp.bfloat16),
        ],
        compiler_params=pltpu.CompilerParams(vmem_limit_bytes=40 << 20),
        name="match",
    )(users, lut, page_count, teacher, picked, pages)


def give_kernel(
    rows_ref, info_ref, out_ref,
    landed, table, parts, r_send, r_recv, t_send, t_recv,
):
    me_g = lax.axis_index("group")
    me_m = lax.axis_index("member")
    barrier = greet(me_g, me_m)
    for s in range(GROUPS):
        for spare in range(CAP, 2 * CAP):
            landed[s, spare] = jnp.zeros((TOK, DIM), jnp.bfloat16)
    pl.semaphore_wait(barrier, MEMBERS - 1 + GROUPS - 1)

    def row_copy(k, src_g):
        peer = (me_g + k) % GROUPS
        return pltpu.make_async_remote_copy(
            src_ref=rows_ref.at[pl.ds(peer * CAP, CAP)],
            dst_ref=landed.at[src_g, pl.ds(0, CAP)],
            send_sem=r_send.at[k],
            recv_sem=r_recv.at[src_g],
            device_id=(peer, me_m),
            device_id_type=MESH,
        )

    def table_copy(k, src_m):
        peer = (me_m + k) % MEMBERS
        return pltpu.make_async_remote_copy(
            src_ref=table.at[k],
            dst_ref=parts.at[src_m],
            send_sem=t_send.at[k],
            recv_sem=t_recv.at[src_m],
            device_id=(me_g, peer),
            device_id_type=MESH,
        )

    for k in (4, 5, 2, 3, 6, 7, 1):
        row_copy(k, me_g).start()
    for n in range(CAP):
        landed[me_g, n] = rows_ref[me_g * CAP + n]
    for k in range(1, GROUPS):
        row_copy(k, (me_g + k) % GROUPS).wait_recv()

    def total_of(owner):
        total = jnp.zeros((TOK, DIM), jnp.float32)
        for s in range(GROUPS):
            total += landed[s, info_ref[s, 0, INV_AT + owner] & (2 * CAP - 1)].astype(jnp.float32)
        return total.astype(jnp.bfloat16)

    def send_table(n, carry):
        k = jnp.where(n >= MEMBERS // 2, n + 1 - MEMBERS // 2, n + MEMBERS // 2)
        table[k] = total_of((me_m + k) % MEMBERS)
        table_copy(k, me_m).start()
        return carry

    lax.fori_loop(0, MEMBERS - 1, send_table, 0)
    parts[me_m] = total_of(me_m)

    def got_part(k, carry):
        table_copy(k, (me_m + k) % MEMBERS).wait_recv()
        return carry

    lax.fori_loop(1, MEMBERS, got_part, 0)
    total = jnp.zeros((TOK, DIM), jnp.float32)
    for m in range(MEMBERS):
        total += parts[m].astype(jnp.float32)
    out_ref[0] = total
    for k in range(1, GROUPS):
        row_copy(k, me_g).wait_send()

    def sent_part(k, carry):
        table_copy(k, me_m).wait_send()
        return carry

    lax.fori_loop(1, MEMBERS, sent_part, 0)


def give(rows, info):
    return pl.pallas_call(
        give_kernel,
        out_shape=jax.ShapeDtypeStruct((1, TOK, DIM), jnp.float32),
        in_specs=[
            pl.BlockSpec(memory_space=pltpu.VMEM),
            pl.BlockSpec(memory_space=pltpu.SMEM),
        ],
        out_specs=pl.BlockSpec(memory_space=pltpu.VMEM),
        scratch_shapes=[
            pltpu.VMEM((GROUPS, 2 * CAP, TOK, DIM), jnp.bfloat16),
            pltpu.VMEM((MEMBERS, TOK, DIM), jnp.bfloat16),
            pltpu.VMEM((MEMBERS, TOK, DIM), jnp.bfloat16),
            pltpu.SemaphoreType.DMA((GROUPS,)),
            pltpu.SemaphoreType.DMA((GROUPS,)),
            pltpu.SemaphoreType.DMA((MEMBERS,)),
            pltpu.SemaphoreType.DMA((MEMBERS,)),
        ],
        compiler_params=pltpu.CompilerParams(collective_id=1, has_side_effects=True),
        name="give",
    )(rows, info)


def body(queries, pages, users, page_count, teacher):
    picked, lut, info = fetch(queries, users)
    scores, rows, page_grad = match(users, lut, page_count, teacher, picked, pages)
    query_grad = give(rows, info)
    return scores, query_grad, page_grad


def solution(mesh):
    both = ("group", "member")
    three, two, one = P(both, None, None), P(both, None), P(both)
    return jax.shard_map(
        body,
        mesh=mesh,
        in_specs=(three, three, two, one, two),
        out_specs=(two, three, three),
        check_vma=False,
    )
```

time: 210 us -> 91.9 us (0.44); the launches traced: 208 us -> 92 us
  Pallas kernels: 0 us -> 84.1 us
  other arithmetic: 48.4 us -> 0 us
  blocking collectives: 45.4 us -> 0 us
  waiting for transfers between devices: 32.8 us -> 0 us
  matrix products: 32.2 us -> 0 us
  local copies, waits for them, and re-layouts: 37 us -> 7.29 us
  starting transfers between devices: 10.8 us -> 0 us
    pallas_call x0 -> x3, Pallas kernels: none -> 84.1 us  [the longest x1 33.9 us: give(): pl.pallas_call(give_kernel, out_shape=jax.ShapeDtypeStruct((1, TOK, DIM),...]
    all_to_all x2 -> x0, blocking collectives: 45.4 us -> none  [the longest x1 29.9 us: sent_to_all(): return lax.all_to_all(copies, axis, split_axis=0, concat_axis=0, tiled=True)]
    all_to_all x2 -> x0, waiting for transfers between devices: 32.8 us -> none  [the longest x1 23.3 us: sent_to_all(): return lax.all_to_all(copies, axis, split_axis=0, concat_axis=0, tiled=True)]
    dot_general x20 -> x0, matrix products: 32.2 us -> none  [the longest x6 10.1 us: page_step(): jnp.dot(rating_gradient_factor, page_tile, preferred_element_type=jnp.flo...]
    convert_element_type x10 -> x0, other arithmetic: 21.8 us -> none  [the longest x6 21.7 us: page_step(): rating_gradient_factor = (mismatch_row_set[:, None] * pairing_coefficient...]
    gather x6 -> x0, local copies, waits for them, and re-layouts: 13.2 us -> none  [page_step(): chosen = gathered[user_row].reshape(slots * tok_rows, width)]
    reduce_sum x21 -> x0, other arithmetic: 12.5 us -> none  [the longest x6 5.84 us: page_step(): aligned_rating = jnp.sum(pairing_coefficients * cosine_affinity, axis=-1)]
    select_n x18 -> x0, other arithmetic: 12 us -> none  [the longest x6 8.06 us: page_step(): unaligned_rating = jnp.where(live, score - teacher_row, 0.0)]
  transfers between devices with their start and end apart: 2 -> 0, of which waited for: 2 -> 0; matrix products, arithmetic and copies ran while one was open for 1% -> 0% of each run, Pallas kernels for 0% -> 0%
where the time goes in v1:
time: 91.9 us; the launch traced here: 92 us
  Pallas kernels  84.1 us (92%)
  local copies, waits for them, and re-layouts  7.29 us (8%)
    pallas_call x1, Pallas kernels, give(): pl.pallas_call(give_kernel, out_shape=jax.ShapeDtypeStruct((1, TOK, DIM),...  33.9 us
    pallas_call x1, Pallas kernels, fetch(): pl.pallas_call(fetch_kernel, out_shape=(jax.ShapeDtypeStruct((GROUPS * CA...  28.7 us
    pallas_call x1, Pallas kernels, match(): pl.pallas_call(match_kernel, out_shape=(jax.ShapeDtypeStruct(users.shape,...  21.4 us
    unnamed x15, local copies, waits for them, and re-layouts  7.29 us

profile of v1, /device:TPU:1, one launch (start us, length us, event | category | flops | bytes accessed | tf_op | source)
XLA Modules:
  0.0 92.0 jit_solution(4175960371638734330)
XLA Ops:
  0.6 28.7 %fetch.1 = (bf16[64,32,128]{2,1,0:T(8,128)(2,1)}, s32[8,256]{1,0:T(8,128)}, s32[8,1,128]{2,1,0:T(1,128)}) custom-call(bf16[1,32,128]{2,1,0:T(8,128)(2,1)} %query_ref.1, s32[6,32]{1,0:T(8,128)} %users_ref.3), custom_call_target="tpu_custom_call" | custom-call | tf_op jit(solution)/shard_map/fetch/pallas_call | solution.py:167
  29.4 0.0 copy-start
  29.4 1.4 %copy-done = bf16[6,1024,128]{2,1,0:T(8,128)(2,1)S(1)} copy-done((bf16[6,1024,128]{2,1,0:T(8,128)(2,1)S(1)}, bf16[6,1024,128]{2,1,0:T(8,128)(2,1)}, u32[]{:S(2)}) %copy-start) | copy-done | bytes 1572888
  30.8 0.0 copy-start.1
  30.8 1.0 %copy-done.1 = bf16[64,32,128]{2,1,0:T(8,128)(2,1)S(1)} copy-done((bf16[64,32,128]{2,1,0:T(8,128)(2,1)S(1)}, bf16[64,32,128]{2,1,0:T(8,128)(2,1)}, u32[]{:S(2)}) %copy-start.1) | copy-done | bytes 524312
  31.8 0.0 copy-start.3
  31.8 0.7 copy-done.3
  32.5 0.0 copy-start.4
  32.5 0.7 copy-done.4
  33.2 0.0 copy-start.5
  33.2 0.7 copy-done.5
  33.9 0.0 copy-start.6
  33.9 0.7 copy-done.6
  34.5 21.4 %match.1 = (f32[6,32]{1,0:T(8,128)}, bf16[64,32,128]{2,1,0:T(8,128)(2,1)S(1)}, bf16[6,1024,128]{2,1,0:T(8,128)(2,1)}) custom-call(s32[6,32]{1,0:T(8,128)S(1)} %copy-done.3, s32[8,256]{1,0:T(8,128)S(1)} %copy-done.4, s32[6]{0:T(128)S(1)} %copy-done.6, f32[6,32]{1,0:T(8,128)S(1)} %copy-done.5, bf16[64,32,128]{2,1,0:T(8,128)(2,1)S(1)} %copy-done.1, ...), custom_call_target="tpu_custom_call" | custom-call | tf_op jit(solution)/shard_map/match/pallas_call | solution.py:345
  56.0 0.0 copy-start.2
  56.0 0.8 copy-done.2
  56.8 33.9 %give.1 = f32[1,32,128]{2,1,0:T(8,128)} custom-call(bf16[64,32,128]{2,1,0:T(8,128)(2,1)} %copy-done.2, s32[8,1,128]{2,1,0:T(1,128)} %get-tuple-element.13.info_ref), custom_call_target="tpu_custom_call" | custom-call | tf_op jit(solution)/shard_map/give/pallas_call | solution.py:447
  90.7 1.3 %copy.9 = f32[1,32,128]{2,1,0:T(8,128)} copy(f32[1,32,128]{2,1,0:T(8,128)} %give.1) | data formatting | bytes 32768
Async XLA Ops:
  29.4 1.4 %copy-start = (bf16[6,1024,128]{2,1,0:T(8,128)(2,1)S(1)}, bf16[6,1024,128]{2,1,0:T(8,128)(2,1)}, u32[]{:S(2)}) copy-start(bf16[6,1024,128]{2,1,0:T(8,128)(2,1)} %pages_ref.1) | copy-start | bytes 4718596
  30.8 1.0 %copy-start.1 = (bf16[64,32,128]{2,1,0:T(8,128)(2,1)S(1)}, bf16[64,32,128]{2,1,0:T(8,128)(2,1)}, u32[]{:S(2)}) copy-start(bf16[64,32,128]{2,1,0:T(8,128)(2,1)} %get-tuple-element.10.picked_ref) | copy-start | bytes 1572868
  31.8 0.7 copy-start.3
  32.5 0.7 copy-start.4
  33.2 0.7 copy-start.5
  33.9 0.7 copy-start.6
  56.0 0.8 copy-start.2

commit v2 on v1

--- a/solution.py
+++ b/solution.py
@@ -19,6 +19,7 @@
 INV_AT = 32
 SCALE = math.log2(math.e) / 0.05
 LN2 = math.log(2.0)
+TOP, PEAK, MASS, MOMENT, BASE, SLANT = range(6)
 
 
 def greet(me_g, me_m):
@@ -39,7 +40,7 @@
 
 
 def fetch_kernel(
-    query_ref, users_ref, picked_ref, lut_ref, info_ref,
+    query_ref, users_ref, picked_ref, place_ref, info_ref,
     table, asks_out, asks_in, asks_smem, chosen,
     q_send, q_recv, a_send, a_recv, c_send, c_recv, local_sem,
 ):
@@ -50,9 +51,8 @@
     total = GROUPS * MEMBERS
     rows = users_ref.shape[0]
     qid = lax.broadcasted_iota(jnp.int32, (total, users_ref.shape[1]), 0)
-    hit = jnp.zeros(qid.shape, jnp.float32)
-    for p in range(rows):
-        hit = jnp.where(users_ref[p : p + 1, :] == qid, 1.0, hit)
+    hits = [jnp.where(users_ref[p : p + 1, :] == qid, 1.0, 0.0) for p in range(rows)]
+    hit = functools.reduce(jnp.maximum, hits)
     count = lax.dot_general(
         jnp.ones((8, users_ref.shape[1]), jnp.bfloat16),
         hit.astype(jnp.bfloat16),
@@ -66,7 +66,13 @@
     rank = jnp.dot(used.astype(jnp.bfloat16), before, preferred_element_type=jnp.float32)
     lane8 = lax.broadcasted_iota(jnp.int32, (8, total), 1)
     sub8 = lax.broadcasted_iota(jnp.int32, (8, total), 0)
-    lut_ref[...] = (lane8 >> 5) * CAP + rank.astype(jnp.int32)
+    spot = ((lane8 >> 5) * CAP).astype(jnp.float32) + rank
+    for p in range(rows):
+        place = jnp.dot(
+            spot.astype(jnp.bfloat16), hits[p].astype(jnp.bfloat16),
+            preferred_element_type=jnp.float32,
+        )
+        place_ref[p : p + 1, :] = place[0:1].astype(jnp.int32)
     of_group = (lane8 >> 5) == sub8
     k_id = lax.broadcasted_iota(jnp.int32, (128, total), 0).astype(jnp.float32)
     local_id = (lax.broadcasted_iota(jnp.int32, (128, total), 1) & 31).astype(jnp.float32)
@@ -168,7 +174,7 @@
         fetch_kernel,
         out_shape=(
             jax.ShapeDtypeStruct((GROUPS * CAP, TOK, DIM), jnp.bfloat16),
-            jax.ShapeDtypeStruct((8, GROUPS * MEMBERS), jnp.int32),
+            jax.ShapeDtypeStruct(users.shape, jnp.int32),
             jax.ShapeDtypeStruct((GROUPS, 1, 128), jnp.int32),
         ),
         in_specs=[pl.BlockSpec(memory_space=pltpu.VMEM)] * 2,
@@ -202,13 +208,23 @@
 
 
 def match_kernel(
-    users_ref, lut_ref, count_ref, teacher_ref, picked_ref, pages_ref,
-    scores_ref, rows_ref, grad_ref,
-    chunks, page_t, sims, logit, expo, stats, acc, row_acc, score_l, same_slot,
+    place_ref, count_ref, teacher_ref, picked_hbm, pages_hbm,
+    scores_ref, rows_ref, grad_hbm,
+    chunks, picked_ref, pages_ref, page_t, sims, logit, expo, stats, acc, grad_ref,
+    row_acc, score_l, same_slot, in_sem, out_sem,
 ):
     n_pages, n_tok, _ = pages_ref.shape
-    per_page = users_ref.shape[1] // CHUNK
-    blocks = n_tok // 256
+    per_page = place_ref.shape[1] // CHUNK
+    half = n_tok // 2
+    quarter = n_tok // 4
+
+    def page_in(p):
+        return pltpu.make_async_copy(pages_hbm.at[p], pages_ref.at[p], in_sem.at[p])
+
+    picked_in = pltpu.make_async_copy(picked_hbm, picked_ref, in_sem.at[n_pages])
+    for p in range(n_pages):
+        page_in(p).start()
+    picked_in.start()
 
     def list_chunk(n, total):
         p = n // per_page
@@ -221,27 +237,31 @@
         return total + alive.astype(jnp.int32)
 
     total = lax.fori_loop(0, n_pages * per_page, list_chunk, 0)
-    chunks[total] = chunks[total - 1]
-    for p in range(n_pages):
-        page_t[p] = pages_ref[p].T
+    for n in range(3):
+        chunks[total + n] = 0
+    pairs = (total + 1) // 2
     acc[...] = jnp.zeros_like(acc)
     row_acc[...] = jnp.zeros_like(row_acc)
     score_l[...] = jnp.zeros_like(score_l)
+    expo[...] = jnp.zeros_like(expo)
+    logit[...] = jnp.zeros_like(logit)
+    stats[...] = jnp.zeros_like(stats)
     seg_r = lax.broadcasted_iota(jnp.int32, (LANES, LANES), 0) >> 5
     seg_c = lax.broadcasted_iota(jnp.int32, (LANES, LANES), 1) >> 5
     same_slot[...] = jnp.where(seg_r == seg_c, 1.0, 0.0).astype(jnp.bfloat16)
     slot_of_lane = lax.broadcasted_iota(jnp.int32, (8, LANES), 1) >> 5
+    for p in range(n_pages):
+        page_in(p).wait()
+        page_t[p] = pages_ref[p].T
+    picked_in.wait()
 
     def where_of(n):
         code = chunks[n]
         return code // per_page, code % per_page
 
-    def picked_at(p, c, k):
-        return lut_ref[0, users_ref[p, c * CHUNK + k]]
-
     def chosen_of(p, c):
         return jnp.concatenate(
-            [picked_ref[picked_at(p, c, k)] for k in range(CHUNK)], axis=0
+            [picked_ref[place_ref[p, c * CHUNK + k]] for k in range(CHUNK)], axis=0
         )
 
     def fold8(value, op):
@@ -253,78 +273,143 @@
             ]
         return parts[0]
 
-    def similar_of(n):
+    def tall(value, rows):
+        return jnp.concatenate([value] * (rows // 8), axis=0)
+
+    def similar_half(p, chosen, slot, h):
+        at = slice(half * h, half * h + half)
+        block = lax.dot_general(
+            pages_ref[p, at, :], chosen, (((1,), (1,)), ((), ())),
+            preferred_element_type=jnp.float32,
+        )
+        sims[slot, at, :] = block
+        return fold8(block, jnp.maximum)
+
+    def similar(n, slot):
         p, c = where_of(n)
         chosen = chosen_of(p, c)
-        top = None
-        for b in range(blocks):
-            block = lax.dot_general(
-                pages_ref[p, 256 * b : 256 * b + 256, :],
-                chosen,
-                (((1,), (1,)), ((), ())),
-                preferred_element_type=jnp.float32,
-            )
-            sims[256 * b : 256 * b + 256, :] = block
-            high = fold8(block, jnp.maximum)
-            top = high if top is None else jnp.maximum(top, high)
-        return jnp.broadcast_to(jnp.max(top, axis=0, keepdims=True), (8, LANES))
-
-    def weigh(top):
-        mass = jnp.zeros((8, LANES), jnp.float32)
-        moment = jnp.zeros((8, LANES), jnp.float32)
-        top64 = jnp.concatenate([top] * 8, axis=0)
-        for b in range(n_tok // 64):
-            at = slice(64 * b, 64 * b + 64)
-            t = (sims[at, :] - top64) * SCALE
+        tops = [similar_half(p, chosen, slot, h) for h in range(2)]
+        stats[slot, TOP] = jnp.maximum(*tops)
+
+    def weigh_rows(slot, top, start, rows):
+        mass = moment = None
+        for i in range(rows // 32):
+            at = slice(start + 32 * i, start + 32 * i + 32)
+            t = sims[slot, at, :] * SCALE - tall(top, 32)
             e = jnp.exp2(t)
-            mass += fold8(e, jnp.add)
-            moment += fold8(e * t, jnp.add)
-            logit[at, :] = t
-            expo[at, :] = e
+            g = e * t
+            logit[slot, at, :] = t
+            expo[slot, at, :] = e
+            e, g = fold8(e, jnp.add), fold8(g, jnp.add)
+            mass = e if mass is None else mass + e
+            moment = g if moment is None else moment + g
         return mass, moment
 
-    def finish(n, top, mass, moment):
+    def settle(n, slot):
         p, c = where_of(n)
-        mass = jnp.broadcast_to(jnp.sum(mass, axis=0, keepdims=True), (8, LANES))
-        moment = jnp.broadcast_to(jnp.sum(moment, axis=0, keepdims=True), (8, LANES))
+        known = n < total
+        mass = jnp.broadcast_to(
+            jnp.sum(stats[slot, MASS], axis=0, keepdims=True), (8, LANES)
+        )
+        moment = jnp.broadcast_to(
+            jnp.sum(stats[slot, MOMENT], axis=0, keepdims=True), (8, LANES)
+        )
         mean = moment / mass
-        matched = top + mean * (1.0 / SCALE)
+        matched = (stats[slot, PEAK] + mean) * (1.0 / SCALE)
         score = split_dot(matched, same_slot[...])
         taught = jnp.zeros((8, LANES), jnp.float32)
         for k in range(CHUNK):
             taught = jnp.where(slot_of_lane == k, teacher_ref[p, c * CHUNK + k], taught)
-        live = slot_of_lane + c * CHUNK < count_ref[p]
-        score_l[c, pl.ds(p, 1), :] = jnp.where(live, score, 0.0)[0:1]
-        part = jnp.where(live, score - taught, 0.0) / mass
+        bound = jnp.where(known, count_ref[p] - c * CHUNK, 0)
+        live = slot_of_lane < bound
+        row = jnp.where(known, p, n_pages)
+        score_l[c, pl.ds(row, 1), :] = jnp.where(live, score, 0.0)[0:1]
+        part = jnp.where(live, (score - taught) / mass, 0.0)
         slant = part * LN2
-        base = part - slant * mean
-        chosen = chosen_of(p, c)
-        base64 = jnp.concatenate([base] * 8, axis=0)
-        slant64 = jnp.concatenate([slant] * 8, axis=0)
-        query_t = jnp.zeros((DIM, LANES), jnp.float32)
-        for b in range(blocks):
-            parts = []
-            for i in range(4):
-                at = slice(256 * b + 64 * i, 256 * b + 64 * i + 64)
-                parts.append(
-                    (expo[at, :] * (base64 + slant64 * logit[at, :])).astype(jnp.bfloat16)
-                )
-            slope = jnp.concatenate(parts, axis=0)
-            at = slice(256 * b, 256 * b + 256)
-            acc[p, at, :] += jnp.dot(slope, chosen, preferred_element_type=jnp.float32)
-            query_t += jnp.dot(page_t[p, :, at], slope, preferred_element_type=jnp.float32)
+        stats[slot, BASE] = part - slant * mean
+        stats[slot, SLANT] = slant
+
+    def slope_rows(slot, base, slant, start, rows):
+        parts = []
+        for i in range(rows // 32):
+            at = slice(start + 32 * i, start + 32 * i + 32)
+            parts.append(
+                (
+                    expo[slot, at, :] * (tall(base, 32) + tall(slant, 32) * logit[slot, at, :])
+                ).astype(jnp.bfloat16)
+            )
+        return jnp.concatenate(parts, axis=0)
+
+    def spread_rows(p, chosen, slope, at, query_t):
+        acc[p, at, :] += jnp.dot(slope, chosen, preferred_element_type=jnp.float32)
+        part = jnp.dot(page_t[p, :, at], slope, preferred_element_type=jnp.float32)
+        return part if query_t is None else query_t + part
+
+    def add_rows(p, c, query_t):
         query_part = query_t.T
         for k in range(CHUNK):
-            row_acc[picked_at(p, c, k)] += query_part[TOK * k : TOK * k + TOK]
-
-    def step(n, carry):
-        top = similar_of(n)
-        mass, moment = weigh(top)
-        finish(n, top, mass, moment)
-        return carry
-
-    lax.fori_loop(0, total, step, 0)
-
+            row_acc[place_ref[p, c * CHUNK + k]] += query_part[TOK * k : TOK * k + TOK]
+
+    def spread(n, slot):
+        p, c = where_of(n)
+        chosen = chosen_of(p, c)
+        base, slant = stats[slot, BASE], stats[slot, SLANT]
+        query_t = None
+        for b in range(4):
+            at = slice(quarter * b, quarter * b + quarter)
+            slope = slope_rows(slot, base, slant, quarter * b, quarter)
+            query_t = spread_rows(p, chosen, slope, at, query_t)
+        add_rows(p, c, query_t)
+
+    def turn(old, now, new, slot):
+        p_old, c_old = where_of(old)
+        p_new, c_new = where_of(new)
+        chosen_old = chosen_of(p_old, c_old)
+        chosen_new = chosen_of(p_new, c_new)
+        base, slant = stats[slot, BASE], stats[slot, SLANT]
+        top = jnp.broadcast_to(
+            jnp.max(stats[slot, TOP], axis=0, keepdims=True), (8, LANES)
+        ) * SCALE
+        stats[slot, PEAK] = top
+        query_t = mass = moment = None
+        tops = []
+        for h in range(2):
+            for b in (2 * h, 2 * h + 1):
+                at = slice(quarter * b, quarter * b + quarter)
+                slope = slope_rows(slot, base, slant, quarter * b, quarter)
+                query_t = spread_rows(p_old, chosen_old, slope, at, query_t)
+                e, g = weigh_rows(slot, top, quarter * b, quarter)
+                mass = e if mass is None else mass + e
+                moment = g if moment is None else moment + g
+            tops.append(similar_half(p_new, chosen_new, slot, h))
+        stats[slot, TOP] = jnp.maximum(*tops)
+        stats[slot, MASS] = mass
+        stats[slot, MOMENT] = moment
+        add_rows(p_old, c_old, query_t)
+
+    similar(0, 0)
+    similar(1, 1)
+
+    def step(i, carry):
+        n = 2 * i
+        old = jnp.maximum(n - 2, 0)
+
+        turn(old, n, n + 2, 0)
+        settle(n, 0)
+        turn(old + 1, n + 1, n + 3, 1)
+        settle(n + 1, 1)
+        return carry
+
+    lax.fori_loop(0, pairs, step, 0)
+    spread(2 * pairs - 2, 0)
+    spread(2 * pairs - 1, 1)
+
+    def page_out(p):
+        return pltpu.make_async_copy(grad_ref.at[p], grad_hbm.at[p], out_sem.at[p])
+
+    for p in range(n_pages):
+        grad_ref[p] = acc[p].astype(jnp.bfloat16)
+        page_out(p).start()
     col = lax.broadcasted_iota(jnp.int32, (LANES, 128), 1)
     row = lax.broadcasted_iota(jnp.int32, (LANES, 128), 0)
     out = jnp.zeros((8, 128), jnp.float32)
@@ -332,40 +417,46 @@
         take = jnp.where(row == (col - c * CHUNK) * TOK, 1.0, 0.0)
         out += split_dot(score_l[c], take.astype(jnp.bfloat16))
     scores_ref[...] = out[: scores_ref.shape[0], : scores_ref.shape[1]]
+    rows_ref[...] = row_acc[...].astype(jnp.bfloat16)
     for p in range(n_pages):
-        grad_ref[p] = acc[p].astype(jnp.bfloat16)
-    rows_ref[...] = row_acc[...].astype(jnp.bfloat16)
-
-
-def match(users, lut, page_count, teacher, picked, pages):
+        page_out(p).wait()
+
+
+def match(place, page_count, teacher, picked, pages):
     n_pages, n_tok, _ = pages.shape
-    per_page = users.shape[1] // CHUNK
+    per_page = teacher.shape[1] // CHUNK
     smem = pl.BlockSpec(memory_space=pltpu.SMEM)
     vmem = pl.BlockSpec(memory_space=pltpu.VMEM)
+    anywhere = pl.BlockSpec(memory_space=pl.ANY)
     return pl.pallas_call(
         match_kernel,
         out_shape=(
-            jax.ShapeDtypeStruct(users.shape, jnp.float32),
+            jax.ShapeDtypeStruct(teacher.shape, jnp.float32),
             jax.ShapeDtypeStruct(picked.shape, jnp.bfloat16),
             jax.ShapeDtypeStruct(pages.shape, jnp.bfloat16),
         ),
-        in_specs=[smem, smem, smem, smem, vmem, vmem],
-        out_specs=[vmem, vmem, vmem],
+        in_specs=[smem, smem, smem, anywhere, anywhere],
+        out_specs=[vmem, vmem, anywhere],
         scratch_shapes=[
-            pltpu.SMEM((n_pages * per_page + 1,), jnp.int32),
+            pltpu.SMEM((n_pages * per_page + 3,), jnp.int32),
+            pltpu.VMEM(picked.shape, jnp.bfloat16),
+            pltpu.VMEM(pages.shape, jnp.bfloat16),
             pltpu.VMEM((n_pages, DIM, n_tok), jnp.bfloat16),
-            pltpu.VMEM((n_tok, LANES), jnp.float32),
-            pltpu.VMEM((n_tok, LANES), jnp.float32),
-            pltpu.VMEM((n_tok, LANES), jnp.float32),
-            pltpu.VMEM((8, LANES), jnp.float32),
+            pltpu.VMEM((2, n_tok, LANES), jnp.float32),
+            pltpu.VMEM((2, n_tok, LANES), jnp.float32),
+            pltpu.VMEM((2, n_tok, LANES), jnp.float32),
+            pltpu.VMEM((2, 6, 8, LANES), jnp.float32),
             pltpu.VMEM((n_pages, n_tok, DIM), jnp.float32),
+            pltpu.VMEM(pages.shape, jnp.bfloat16),
             pltpu.VMEM(picked.shape, jnp.float32),
             pltpu.VMEM((per_page, 8, LANES), jnp.float32),
             pltpu.VMEM((LANES, LANES), jnp.bfloat16),
+            pltpu.SemaphoreType.DMA((n_pages + 1,)),
+            pltpu.SemaphoreType.DMA((n_pages,)),
         ],
-        compiler_params=pltpu.CompilerParams(vmem_limit_bytes=40 << 20),
+        compiler_params=pltpu.CompilerParams(vmem_limit_bytes=60 * 1024 * 1024),
         name="match",
-    )(users, lut, page_count, teacher, picked, pages)
+    )(place, page_count, teacher, picked, pages)
 
 
 def give_kernel(
@@ -467,8 +558,8 @@
 
 
 def body(queries, pages, users, page_count, teacher):
-    picked, lut, info = fetch(queries, users)
-    scores, rows, page_grad = match(users, lut, page_count, teacher, picked, pages)
+    picked, place, info = fetch(queries, users)
+    scores, rows, page_grad = match(place, page_count, teacher, picked, pages)
     query_grad = give(rows, info)
     return scores, query_grad, page_grad
 

time: 91.9 us -> 73.8 us (0.80)
  Pallas kernels: 84.1 us -> 71.5 us
  local copies, waits for them, and re-layouts: 7.29 us -> 1.32 us
    pallas_call x1, Pallas kernels: 21.4 us -> 12.8 us  [match(): pl.pallas_call(match_kernel, out_shape=(jax.ShapeDtypeStruct(teacher.shap...]
    unnamed x15 -> x1, local copies, waits for them, and re-layouts: 7.29 us -> 1.32 us
    pallas_call x1, Pallas kernels: 33.9 us -> 30 us  [give(): pl.pallas_call(give_kernel, out_shape=jax.ShapeDtypeStruct((1, TOK, DIM),...]
where the time goes in v2:
time: 73.8 us; the launch traced here: 73.5 us
  Pallas kernels  71.5 us (97%)
  local copies, waits for them, and re-layouts  1.32 us (2%)
    pallas_call x1, Pallas kernels, give(): pl.pallas_call(give_kernel, out_shape=jax.ShapeDtypeStruct((1, TOK, DIM),...  30 us
    pallas_call x1, Pallas kernels, fetch(): pl.pallas_call(fetch_kernel, out_shape=(jax.ShapeDtypeStruct((GROUPS * CA...  28.7 us
    pallas_call x1, Pallas kernels, match(): pl.pallas_call(match_kernel, out_shape=(jax.ShapeDtypeStruct(teacher.shap...  12.8 us

profile of v2, /device:TPU:1, one launch (start us, length us, event | category | flops | bytes accessed | tf_op | source)
XLA Modules:
  0.0 73.5 jit_solution(11860843475939942858)
XLA Ops:
  0.6 28.7 %fetch.1 = (bf16[64,32,128]{2,1,0:T(8,128)(2,1)}, s32[6,32]{1,0:T(8,128)}, s32[8,1,128]{2,1,0:T(1,128)}) custom-call(bf16[1,32,128]{2,1,0:T(8,128)(2,1)} %query_ref.1, s32[6,32]{1,0:T(8,128)} %users_ref.1), custom_call_target="tpu_custom_call" | custom-call | tf_op jit(solution)/shard_map/fetch/pallas_call | solution.py:173
  29.4 12.8 %match.1 = (f32[6,32]{1,0:T(8,128)}, bf16[64,32,128]{2,1,0:T(8,128)(2,1)}, bf16[6,1024,128]{2,1,0:T(8,128)(2,1)}) custom-call(s32[6,32]{1,0:T(8,128)} %get-tuple-element.9.place_ref, s32[6]{0:T(128)} %count_ref.1, f32[6,32]{1,0:T(8,128)} %teacher_ref.1, bf16[64,32,128]{2,1,0:T(8,128)(2,1)} %get-tuple-element.10.picked_hbm, bf16[6,1024,128]{2,1,0:T(8,128)(2,1)} %pages_hbm.1), custom_call_target="tpu_custom_call" | custom-call | tf_op jit(solution)/shard_map/match/pallas_call | solution.py:431
  42.1 30.0 %give.1 = f32[1,32,128]{2,1,0:T(8,128)} custom-call(bf16[64,32,128]{2,1,0:T(8,128)(2,1)} %get-tuple-element.12.rows_ref, s32[8,1,128]{2,1,0:T(1,128)} %get-tuple-element.13.info_ref), custom_call_target="tpu_custom_call" | custom-call | tf_op jit(solution)/shard_map/give/pallas_call | solution.py:538
  72.2 1.3 %copy.9 = f32[1,32,128]{2,1,0:T(8,128)} copy(f32[1,32,128]{2,1,0:T(8,128)} %give.1) | data formatting | bytes 32768

commit v3 on v2

--- a/solution.py
+++ b/solution.py
@@ -13,6 +13,10 @@
 GROUPS = 8
 MEMBERS = 32
 TOK = 32
+ZS, YS = 8, 4
+Z_FAR = (4, 3, 5, 2, 6, 1, 7)
+Z_NEAR = (1, 7, 2, 6, 3, 5, 4)
+Y_FAR = (2, 1, 3)
 DIM = 128
 CHUNK = 8
 LANES = CHUNK * TOK
@@ -22,31 +26,43 @@
 TOP, PEAK, MASS, MOMENT, BASE, SLANT = range(6)
 
 
+def along(me_m, dz, dy):
+    return ((me_m // YS + dz) % ZS) * YS + (me_m % YS + dy) % YS
+
+
 def greet(me_g, me_m):
     barrier = pltpu.get_barrier_semaphore()
-
-    def to_member(k, carry):
-        pl.semaphore_signal(
-            barrier, inc=1, device_id=(me_g, (me_m + k) % MEMBERS), device_id_type=MESH
-        )
-        return carry
-
-    lax.fori_loop(1, MEMBERS, to_member, 0)
-    for k in range(1, GROUPS):
-        pl.semaphore_signal(
-            barrier, inc=1, device_id=((me_g + k) % GROUPS, me_m), device_id_type=MESH
-        )
-    return barrier
+    peers = [(me_g, along(me_m, k, 0)) for k in Z_FAR]
+    peers += [(me_g, along(me_m, 0, k)) for k in range(1, YS)]
+    peers += [((me_g + k) % GROUPS, me_m) for k in range(1, GROUPS)]
+    for peer in peers:
+        pl.semaphore_signal(barrier, inc=1, device_id=peer, device_id_type=MESH)
+    return barrier, len(peers)
 
 
 def fetch_kernel(
-    query_ref, users_ref, picked_ref, place_ref, info_ref,
-    table, asks_out, asks_in, asks_smem, chosen,
-    q_send, q_recv, a_send, a_recv, c_send, c_recv, local_sem,
+    query_hbm, users_hbm, pages_hbm, picked_hbm, place_ref, info_ref, page_t_hbm,
+    table, users_ref, pages_ref, page_t, asks_out, asks_in, asks_smem, chosen,
+    z_send, y_send, q_recv, a_send, a_recv, c_send, c_recv, local_sem, in_sem, out_sem,
 ):
     me_g = lax.axis_index("group")
     me_m = lax.axis_index("member")
-    barrier = greet(me_g, me_m)
+    n_pages = pages_hbm.shape[0]
+    barrier, greeted = greet(me_g, me_m)
+    users_in = pltpu.make_async_copy(users_hbm, users_ref, local_sem.at[0])
+    query_in = pltpu.make_async_copy(query_hbm.at[0], table.at[me_m], local_sem.at[1])
+    users_in.start()
+    query_in.start()
+
+    def page_in(p):
+        return pltpu.make_async_copy(pages_hbm.at[p], pages_ref.at[p], in_sem.at[p])
+
+    def page_out(p):
+        return pltpu.make_async_copy(page_t.at[p], page_t_hbm.at[p], out_sem.at[p])
+
+    for p in range(n_pages):
+        page_in(p).start()
+    users_in.wait()
 
     total = GROUPS * MEMBERS
     rows = users_ref.shape[0]
@@ -66,13 +82,6 @@
     rank = jnp.dot(used.astype(jnp.bfloat16), before, preferred_element_type=jnp.float32)
     lane8 = lax.broadcasted_iota(jnp.int32, (8, total), 1)
     sub8 = lax.broadcasted_iota(jnp.int32, (8, total), 0)
-    spot = ((lane8 >> 5) * CAP).astype(jnp.float32) + rank
-    for p in range(rows):
-        place = jnp.dot(
-            spot.astype(jnp.bfloat16), hits[p].astype(jnp.bfloat16),
-            preferred_element_type=jnp.float32,
-        )
-        place_ref[p : p + 1, :] = place[0:1].astype(jnp.int32)
     of_group = (lane8 >> 5) == sub8
     k_id = lax.broadcasted_iota(jnp.int32, (128, total), 0).astype(jnp.float32)
     local_id = (lax.broadcasted_iota(jnp.int32, (128, total), 1) & 31).astype(jnp.float32)
@@ -91,111 +100,136 @@
     asks = (ids + spread).astype(jnp.int32)
     for g in range(GROUPS):
         asks_out[g] = asks[g : g + 1, :]
-
-    pl.semaphore_wait(barrier, MEMBERS - 1 + GROUPS - 1)
-
-    def query_copy(k, src_m):
-        peer = (me_m + k) % MEMBERS
+    query_in.wait()
+
+    def remote(src, dst, send, recv, g, m):
         return pltpu.make_async_remote_copy(
-            src_ref=query_ref.at[0],
-            dst_ref=table.at[src_m],
-            send_sem=q_send.at[k],
-            recv_sem=q_recv.at[src_m],
-            device_id=(me_g, peer),
-            device_id_type=MESH,
+            src_ref=src, dst_ref=dst, send_sem=send, recv_sem=recv,
+            device_id=(g, m), device_id_type=MESH,
+        )
+
+    def z_copy(k, src_m):
+        return remote(
+            table.at[src_m], table.at[src_m], z_send.at[k], q_recv.at[src_m],
+            me_g, along(me_m, k, 0),
+        )
+
+    def y_copy(k, j, src_m):
+        return remote(
+            table.at[src_m], table.at[src_m], y_send.at[YS * k + j], q_recv.at[src_m],
+            me_g, along(me_m, 0, j),
         )
 
     def ask_copy(k, src_g):
         peer = (me_g + k) % GROUPS
-        return pltpu.make_async_remote_copy(
-            src_ref=asks_out.at[peer],
-            dst_ref=asks_in.at[src_g],
-            send_sem=a_send.at[k],
-            recv_sem=a_recv.at[src_g],
-            device_id=(peer, me_m),
-            device_id_type=MESH,
+        return remote(
+            asks_out.at[peer], asks_in.at[src_g], a_send.at[k], a_recv.at[src_g], peer, me_m
         )
 
     def chosen_copy(k, src_g):
         peer = (me_g + k) % GROUPS
-        return pltpu.make_async_remote_copy(
-            src_ref=chosen.at[k],
-            dst_ref=picked_ref.at[pl.ds(src_g * CAP, CAP)],
-            send_sem=c_send.at[k],
-            recv_sem=c_recv.at[src_g],
-            device_id=(peer, me_m),
-            device_id_type=MESH,
-        )
-
+        return remote(
+            chosen.at[k], picked_hbm.at[pl.ds(src_g * CAP, CAP)],
+            c_send.at[k], c_recv.at[src_g], peer, me_m,
+        )
+
+    pl.semaphore_wait(barrier, greeted)
+    for k in Z_FAR:
+        z_copy(k, me_m).start()
+    for j in Y_FAR:
+        y_copy(0, j, me_m).start()
     for k in range(1, GROUPS):
         ask_copy(k, me_g).start()
-
-    def send_query(k, carry):
-        query_copy(k, me_m).start()
-        return carry
-
-    lax.fori_loop(1, MEMBERS, send_query, 0)
-    table[me_m] = query_ref[0]
     asks_in[me_g] = asks_out[me_g]
+    spot = ((lane8 >> 5) * CAP).astype(jnp.float32) + rank
+    for p in range(rows):
+        place = jnp.dot(
+            spot.astype(jnp.bfloat16), hits[p].astype(jnp.bfloat16),
+            preferred_element_type=jnp.float32,
+        )
+        place_ref[p : p + 1, :] = place[0:1].astype(jnp.int32)
+    for p in range(n_pages):
+        page_in(p).wait()
+        page_t[p] = pages_ref[p].T
+        page_out(p).start()
+    for k in Z_NEAR:
+        src = along(me_m, k, 0)
+        z_copy(k, src).wait_recv()
+        for j in Y_FAR:
+            y_copy(k, j, src).start()
     for k in range(1, GROUPS):
         ask_copy(k, (me_g + k) % GROUPS).wait_recv()
-    to_smem = pltpu.make_async_copy(asks_in, asks_smem, local_sem)
+    to_smem = pltpu.make_async_copy(asks_in, asks_smem, local_sem.at[0])
     to_smem.start()
     info_ref[...] = asks_in[...]
     to_smem.wait()
-
-    def got_query(k, carry):
-        query_copy(k, (me_m + k) % MEMBERS).wait_recv()
-        return carry
-
-    lax.fori_loop(1, MEMBERS, got_query, 0)
-    for k in (4, 5, 2, 3, 6, 7, 1):
+    for k in (0,) + Z_NEAR:
+        for j in range(1, YS):
+            y_copy(k, j, along(me_m, k, j)).wait_recv()
+
+    for k in (4, 5, 2, 3, 6, 7, 1, 0):
         peer = (me_g + k) % GROUPS
         for n in range(CAP):
             chosen[k, n] = table[asks_smem[peer, 0, n] & (MEMBERS - 1)]
-        chosen_copy(k, me_g).start()
-    for n in range(CAP):
-        picked_ref[me_g * CAP + n] = table[asks_smem[me_g, 0, n] & (MEMBERS - 1)]
+        if k:
+            chosen_copy(k, me_g).start()
+    own = pltpu.make_async_copy(
+        chosen.at[0], picked_hbm.at[pl.ds(me_g * CAP, CAP)], local_sem.at[1]
+    )
+    own.start()
+    for p in range(n_pages):
+        page_out(p).wait()
+    for k in Z_NEAR:
+        z_copy(k, me_m).wait_send()
+    for k in (0,) + Z_NEAR:
+        for j in range(1, YS):
+            y_copy(k, j, along(me_m, k, 0)).wait_send()
+    own.wait()
     for k in range(1, GROUPS):
         chosen_copy(k, (me_g + k) % GROUPS).wait_recv()
-    for k in range(1, GROUPS):
         ask_copy(k, me_g).wait_send()
         chosen_copy(k, me_g).wait_send()
 
-    def sent_query(k, carry):
-        query_copy(k, me_m).wait_send()
-        return carry
-
-    lax.fori_loop(1, MEMBERS, sent_query, 0)
-
-
-def fetch(queries, users):
+
+def fetch(queries, users, pages):
+    n_pages, n_tok, _ = pages.shape
+    vmem = pl.BlockSpec(memory_space=pltpu.VMEM)
+    anywhere = pl.BlockSpec(memory_space=pl.ANY)
     return pl.pallas_call(
         fetch_kernel,
         out_shape=(
             jax.ShapeDtypeStruct((GROUPS * CAP, TOK, DIM), jnp.bfloat16),
             jax.ShapeDtypeStruct(users.shape, jnp.int32),
             jax.ShapeDtypeStruct((GROUPS, 1, 128), jnp.int32),
+            jax.ShapeDtypeStruct((n_pages, DIM, n_tok), jnp.bfloat16),
         ),
-        in_specs=[pl.BlockSpec(memory_space=pltpu.VMEM)] * 2,
-        out_specs=[pl.BlockSpec(memory_space=pltpu.VMEM)] * 3,
+        in_specs=[anywhere] * 3,
+        out_specs=[anywhere, vmem, vmem, anywhere],
         scratch_shapes=[
             pltpu.VMEM((MEMBERS, TOK, DIM), jnp.bfloat16),
+            pltpu.VMEM(users.shape, jnp.int32),
+            pltpu.VMEM(pages.shape, jnp.bfloat16),
+            pltpu.VMEM((n_pages, DIM, n_tok), jnp.bfloat16),
             pltpu.VMEM((GROUPS, 1, 128), jnp.int32),
             pltpu.VMEM((GROUPS, 1, 128), jnp.int32),
             pltpu.SMEM((GROUPS, 1, 128), jnp.int32),
             pltpu.VMEM((GROUPS, CAP, TOK, DIM), jnp.bfloat16),
+            pltpu.SemaphoreType.DMA((ZS,)),
             pltpu.SemaphoreType.DMA((MEMBERS,)),
             pltpu.SemaphoreType.DMA((MEMBERS,)),
             pltpu.SemaphoreType.DMA((GROUPS,)),
             pltpu.SemaphoreType.DMA((GROUPS,)),
             pltpu.SemaphoreType.DMA((GROUPS,)),
             pltpu.SemaphoreType.DMA((GROUPS,)),
-            pltpu.SemaphoreType.DMA,
+            pltpu.SemaphoreType.DMA((2,)),
+            pltpu.SemaphoreType.DMA((n_pages,)),
+            pltpu.SemaphoreType.DMA((n_pages,)),
         ],
-        compiler_params=pltpu.CompilerParams(collective_id=0, has_side_effects=True),
+        compiler_params=pltpu.CompilerParams(
+            collective_id=0, has_side_effects=True, vmem_limit_bytes=60 * 1024 * 1024
+        ),
         name="fetch",
-    )(queries, users)
+    )(queries, users, pages)
 
 
 def split_dot(value, ones):
@@ -208,10 +242,10 @@
 
 
 def match_kernel(
-    place_ref, count_ref, teacher_ref, picked_hbm, pages_hbm,
+    place_ref, count_ref, teacher_ref, picked_hbm, pages_hbm, page_t_hbm,
     scores_ref, rows_ref, grad_hbm,
-    chunks, picked_ref, pages_ref, page_t, sims, logit, expo, stats, acc, grad_ref,
-    row_acc, score_l, same_slot, in_sem, out_sem,
+    chunks, picked_ref, scaled, pages_ref, page_t, sims, logit, expo, stats, acc,
+    grad_ref, row_acc, score_l, same_slot, in_sem, out_sem,
 ):
     n_pages, n_tok, _ = pages_ref.shape
     per_page = place_ref.shape[1] // CHUNK
@@ -222,9 +256,11 @@
         return pltpu.make_async_copy(pages_hbm.at[p], pages_ref.at[p], in_sem.at[p])
 
     picked_in = pltpu.make_async_copy(picked_hbm, picked_ref, in_sem.at[n_pages])
+    turned_in = pltpu.make_async_copy(page_t_hbm, page_t, in_sem.at[n_pages + 1])
+    picked_in.start()
     for p in range(n_pages):
         page_in(p).start()
-    picked_in.start()
+    turned_in.start()
 
     def list_chunk(n, total):
         p = n // per_page
@@ -250,18 +286,27 @@
     seg_c = lax.broadcasted_iota(jnp.int32, (LANES, LANES), 1) >> 5
     same_slot[...] = jnp.where(seg_r == seg_c, 1.0, 0.0).astype(jnp.bfloat16)
     slot_of_lane = lax.broadcasted_iota(jnp.int32, (8, LANES), 1) >> 5
+    picked_in.wait()
+
+    def scale_picked(n, carry):
+        full = picked_ref[n].astype(jnp.float32) * SCALE
+        high = full.astype(jnp.bfloat16)
+        scaled[n, :, :DIM] = high
+        scaled[n, :, DIM:] = (full - high.astype(jnp.float32)).astype(jnp.bfloat16)
+        return carry
+
+    lax.fori_loop(0, picked_ref.shape[0], scale_picked, 0, unroll=8)
     for p in range(n_pages):
         page_in(p).wait()
-        page_t[p] = pages_ref[p].T
-    picked_in.wait()
+    turned_in.wait()
 
     def where_of(n):
         code = chunks[n]
         return code // per_page, code % per_page
 
-    def chosen_of(p, c):
+    def chosen_of(p, c, source):
         return jnp.concatenate(
-            [picked_ref[place_ref[p, c * CHUNK + k]] for k in range(CHUNK)], axis=0
+            [source[place_ref[p, c * CHUNK + k]] for k in range(CHUNK)], axis=0
         )
 
     def fold8(value, op):
@@ -278,8 +323,9 @@
 
     def similar_half(p, chosen, slot, h):
         at = slice(half * h, half * h + half)
+        page = pages_ref[p, at, :]
         block = lax.dot_general(
-            pages_ref[p, at, :], chosen, (((1,), (1,)), ((), ())),
+            jnp.concatenate([page, page], axis=1), chosen, (((1,), (1,)), ((), ())),
             preferred_element_type=jnp.float32,
         )
         sims[slot, at, :] = block
@@ -287,7 +333,7 @@
 
     def similar(n, slot):
         p, c = where_of(n)
-        chosen = chosen_of(p, c)
+        chosen = chosen_of(p, c, scaled)
         tops = [similar_half(p, chosen, slot, h) for h in range(2)]
         stats[slot, TOP] = jnp.maximum(*tops)
 
@@ -295,7 +341,7 @@
         mass = moment = None
         for i in range(rows // 32):
             at = slice(start + 32 * i, start + 32 * i + 32)
-            t = sims[slot, at, :] * SCALE - tall(top, 32)
+            t = sims[slot, at, :] - tall(top, 32)
             e = jnp.exp2(t)
             g = e * t
             logit[slot, at, :] = t
@@ -333,10 +379,9 @@
         parts = []
         for i in range(rows // 32):
             at = slice(start + 32 * i, start + 32 * i + 32)
+            t = logit[slot, at, :]
             parts.append(
-                (
-                    expo[slot, at, :] * (tall(base, 32) + tall(slant, 32) * logit[slot, at, :])
-                ).astype(jnp.bfloat16)
+                (expo[slot, at, :] * (tall(base, 32) + tall(slant, 32) * t)).astype(jnp.bfloat16)
             )
         return jnp.concatenate(parts, axis=0)
 
@@ -352,7 +397,7 @@
 
     def spread(n, slot):
         p, c = where_of(n)
-        chosen = chosen_of(p, c)
+        chosen = chosen_of(p, c, picked_ref)
         base, slant = stats[slot, BASE], stats[slot, SLANT]
         query_t = None
         for b in range(4):
@@ -364,12 +409,12 @@
     def turn(old, now, new, slot):
         p_old, c_old = where_of(old)
         p_new, c_new = where_of(new)
-        chosen_old = chosen_of(p_old, c_old)
-        chosen_new = chosen_of(p_new, c_new)
+        chosen_old = chosen_of(p_old, c_old, picked_ref)
+        chosen_new = chosen_of(p_new, c_new, scaled)
         base, slant = stats[slot, BASE], stats[slot, SLANT]
         top = jnp.broadcast_to(
             jnp.max(stats[slot, TOP], axis=0, keepdims=True), (8, LANES)
-        ) * SCALE
+        )
         stats[slot, PEAK] = top
         query_t = mass = moment = None
         tops = []
@@ -422,7 +467,7 @@
         page_out(p).wait()
 
 
-def match(place, page_count, teacher, picked, pages):
+def match(place, page_count, teacher, picked, pages, page_t):
     n_pages, n_tok, _ = pages.shape
     per_page = teacher.shape[1] // CHUNK
     smem = pl.BlockSpec(memory_space=pltpu.SMEM)
@@ -435,11 +480,12 @@
             jax.ShapeDtypeStruct(picked.shape, jnp.bfloat16),
             jax.ShapeDtypeStruct(pages.shape, jnp.bfloat16),
         ),
-        in_specs=[smem, smem, smem, anywhere, anywhere],
+        in_specs=[smem, smem, smem, anywhere, anywhere, anywhere],
         out_specs=[vmem, vmem, anywhere],
         scratch_shapes=[
             pltpu.SMEM((n_pages * per_page + 3,), jnp.int32),
             pltpu.VMEM(picked.shape, jnp.bfloat16),
+            pltpu.VMEM((GROUPS * CAP, TOK, 2 * DIM), jnp.bfloat16),
             pltpu.VMEM(pages.shape, jnp.bfloat16),
             pltpu.VMEM((n_pages, DIM, n_tok), jnp.bfloat16),
             pltpu.VMEM((2, n_tok, LANES), jnp.float32),
@@ -451,87 +497,96 @@
             pltpu.VMEM(picked.shape, jnp.float32),
             pltpu.VMEM((per_page, 8, LANES), jnp.float32),
             pltpu.VMEM((LANES, LANES), jnp.bfloat16),
-            pltpu.SemaphoreType.DMA((n_pages + 1,)),
+            pltpu.SemaphoreType.DMA((n_pages + 2,)),
             pltpu.SemaphoreType.DMA((n_pages,)),
         ],
         compiler_params=pltpu.CompilerParams(vmem_limit_bytes=60 * 1024 * 1024),
         name="match",
-    )(place, page_count, teacher, picked, pages)
+    )(place, page_count, teacher, picked, pages, page_t)
 
 
 def give_kernel(
-    rows_ref, info_ref, out_ref,
-    landed, table, parts, r_send, r_recv, t_send, t_recv,
+    rows_hbm, info_ref, out_ref,
+    rows_ref, landed, table, y_parts, z_sums, z_parts,
+    r_send, r_recv, y_send, y_recv, z_send, z_recv, local_sem,
 ):
     me_g = lax.axis_index("group")
     me_m = lax.axis_index("member")
-    barrier = greet(me_g, me_m)
+    barrier, greeted = greet(me_g, me_m)
+    rows_in = pltpu.make_async_copy(rows_hbm, rows_ref, local_sem)
+    rows_in.start()
     for s in range(GROUPS):
         for spare in range(CAP, 2 * CAP):
             landed[s, spare] = jnp.zeros((TOK, DIM), jnp.bfloat16)
-    pl.semaphore_wait(barrier, MEMBERS - 1 + GROUPS - 1)
+    rows_in.wait()
+    for n in range(CAP):
+        landed[me_g, n] = rows_ref[me_g * CAP + n]
+    pl.semaphore_wait(barrier, greeted)
+
+    def remote(src, dst, send, recv, g, m):
+        return pltpu.make_async_remote_copy(
+            src_ref=src, dst_ref=dst, send_sem=send, recv_sem=recv,
+            device_id=(g, m), device_id_type=MESH,
+        )
 
     def row_copy(k, src_g):
         peer = (me_g + k) % GROUPS
-        return pltpu.make_async_remote_copy(
-            src_ref=rows_ref.at[pl.ds(peer * CAP, CAP)],
-            dst_ref=landed.at[src_g, pl.ds(0, CAP)],
-            send_sem=r_send.at[k],
-            recv_sem=r_recv.at[src_g],
-            device_id=(peer, me_m),
-            device_id_type=MESH,
-        )
-
-    def table_copy(k, src_m):
-        peer = (me_m + k) % MEMBERS
-        return pltpu.make_async_remote_copy(
-            src_ref=table.at[k],
-            dst_ref=parts.at[src_m],
-            send_sem=t_send.at[k],
-            recv_sem=t_recv.at[src_m],
-            device_id=(me_g, peer),
-            device_id_type=MESH,
+        return remote(
+            rows_ref.at[pl.ds(peer * CAP, CAP)], landed.at[src_g, pl.ds(0, CAP)],
+            r_send.at[k], r_recv.at[src_g], peer, me_m,
+        )
+
+    def y_copy(k, j, slot):
+        return remote(
+            table.at[YS * k + j], y_parts.at[YS * k + slot],
+            y_send.at[YS * k + j], y_recv.at[YS * k + slot], me_g, along(me_m, 0, j),
+        )
+
+    def z_copy(k, slot):
+        return remote(
+            z_sums.at[k], z_parts.at[slot], z_send.at[k], z_recv.at[slot],
+            me_g, along(me_m, k, 0),
         )
 
     for k in (4, 5, 2, 3, 6, 7, 1):
         row_copy(k, me_g).start()
-    for n in range(CAP):
-        landed[me_g, n] = rows_ref[me_g * CAP + n]
     for k in range(1, GROUPS):
         row_copy(k, (me_g + k) % GROUPS).wait_recv()
 
     def total_of(owner):
         total = jnp.zeros((TOK, DIM), jnp.float32)
         for s in range(GROUPS):
-            total += landed[s, info_ref[s, 0, INV_AT + owner] & (2 * CAP - 1)].astype(jnp.float32)
-        return total.astype(jnp.bfloat16)
-
-    def send_table(n, carry):
-        k = jnp.where(n >= MEMBERS // 2, n + 1 - MEMBERS // 2, n + MEMBERS // 2)
-        table[k] = total_of((me_m + k) % MEMBERS)
-        table_copy(k, me_m).start()
-        return carry
-
-    lax.fori_loop(0, MEMBERS - 1, send_table, 0)
-    parts[me_m] = total_of(me_m)
-
-    def got_part(k, carry):
-        table_copy(k, (me_m + k) % MEMBERS).wait_recv()
-        return carry
-
-    lax.fori_loop(1, MEMBERS, got_part, 0)
-    total = jnp.zeros((TOK, DIM), jnp.float32)
-    for m in range(MEMBERS):
-        total += parts[m].astype(jnp.float32)
-    out_ref[0] = total
+            total += landed[s, info_ref[s, 0, INV_AT + owner] & (2 * CAP - 1)].astype(
+                jnp.float32
+            )
+        return total
+
+    for k in Z_FAR + (0,):
+        for j in Y_FAR:
+            table[YS * k + j] = total_of(along(me_m, k, j)).astype(jnp.bfloat16)
+            y_copy(k, j, YS - j).start()
+    mine = None
+    for k in Z_FAR + (0,):
+        total = total_of(along(me_m, k, 0))
+        for j in (1, 3, 2):
+            y_copy(k, j, j).wait_recv()
+            total += y_parts[YS * k + j].astype(jnp.float32)
+        if k:
+            z_sums[k] = total.astype(jnp.bfloat16)
+            z_copy(k, ZS - k).start()
+        else:
+            mine = total
+    for k in Z_NEAR:
+        z_copy(k, k).wait_recv()
+        mine += z_parts[k].astype(jnp.float32)
+    out_ref[0] = mine
     for k in range(1, GROUPS):
         row_copy(k, me_g).wait_send()
-
-    def sent_part(k, carry):
-        table_copy(k, me_m).wait_send()
-        return carry
-
-    lax.fori_loop(1, MEMBERS, sent_part, 0)
+    for k in range(ZS):
+        for j in range(1, YS):
+            y_copy(k, j, j).wait_send()
+        if k:
+            z_copy(k, k).wait_send()
 
 
 def give(rows, info):
@@ -539,27 +594,35 @@
         give_kernel,
         out_shape=jax.ShapeDtypeStruct((1, TOK, DIM), jnp.float32),
         in_specs=[
-            pl.BlockSpec(memory_space=pltpu.VMEM),
+            pl.BlockSpec(memory_space=pl.ANY),
             pl.BlockSpec(memory_space=pltpu.SMEM),
         ],
         out_specs=pl.BlockSpec(memory_space=pltpu.VMEM),
         scratch_shapes=[
+            pltpu.VMEM((GROUPS * CAP, TOK, DIM), jnp.bfloat16),
             pltpu.VMEM((GROUPS, 2 * CAP, TOK, DIM), jnp.bfloat16),
             pltpu.VMEM((MEMBERS, TOK, DIM), jnp.bfloat16),
             pltpu.VMEM((MEMBERS, TOK, DIM), jnp.bfloat16),
+            pltpu.VMEM((ZS, TOK, DIM), jnp.bfloat16),
+            pltpu.VMEM((ZS, TOK, DIM), jnp.bfloat16),
             pltpu.SemaphoreType.DMA((GROUPS,)),
             pltpu.SemaphoreType.DMA((GROUPS,)),
             pltpu.SemaphoreType.DMA((MEMBERS,)),
             pltpu.SemaphoreType.DMA((MEMBERS,)),
+            pltpu.SemaphoreType.DMA((ZS,)),
+            pltpu.SemaphoreType.DMA((ZS,)),
+            pltpu.SemaphoreType.DMA,
         ],
-        compiler_params=pltpu.CompilerParams(collective_id=1, has_side_effects=True),
+        compiler_params=pltpu.CompilerParams(
+            collective_id=1, has_side_effects=True, vmem_limit_bytes=60 * 1024 * 1024
+        ),
         name="give",
     )(rows, info)
 
 
 def body(queries, pages, users, page_count, teacher):
-    picked, place, info = fetch(queries, users)
-    scores, rows, page_grad = match(place, page_count, teacher, picked, pages)
+    picked, place, info, page_t = fetch(queries, users, pages)
+    scores, rows, page_grad = match(place, page_count, teacher, picked, pages, page_t)
     query_grad = give(rows, info)
     return scores, query_grad, page_grad
 

time: 73.8 us -> 65.1 us (0.88)
  Pallas kernels: 71.5 us -> 62.8 us
    pallas_call x1, Pallas kernels: 30 us -> 23.4 us  [give(): pl.pallas_call(give_kernel, out_shape=jax.ShapeDtypeStruct((1, TOK, DIM),...]
    pallas_call x1, Pallas kernels: 28.7 us -> 26.2 us  [fetch(): pl.pallas_call(fetch_kernel, out_shape=(jax.ShapeDtypeStruct((GROUPS * CA...]
where the time goes in v3:
time: 65.1 us; the launch traced here: 64.7 us
  Pallas kernels  62.8 us (96%)
  local copies, waits for them, and re-layouts  1.32 us (2%)
    pallas_call x1, Pallas kernels, fetch(): pl.pallas_call(fetch_kernel, out_shape=(jax.ShapeDtypeStruct((GROUPS * CA...  26.2 us
    pallas_call x1, Pallas kernels, give(): pl.pallas_call(give_kernel, out_shape=jax.ShapeDtypeStruct((1, TOK, DIM),...  23.4 us
    pallas_call x1, Pallas kernels, match(): pl.pallas_call(match_kernel, out_shape=(jax.ShapeDtypeStruct(teacher.shap...  13.2 us
    unnamed x1, local copies, waits for them, and re-layouts  1.32 us

profile of v3, /device:TPU:1, one launch (start us, length us, event | category | flops | bytes accessed | tf_op | source)
XLA Modules:
  0.0 64.7 jit_solution(7431546553207039755)
XLA Ops:
  0.6 26.2 %fetch.1 = (bf16[64,32,128]{2,1,0:T(8,128)(2,1)}, s32[6,32]{1,0:T(8,128)}, s32[8,1,128]{2,1,0:T(1,128)}, bf16[6,128,1024]{2,1,0:T(8,128)(2,1)}) custom-call(bf16[1,32,128]{2,1,0:T(8,128)(2,1)} %query_hbm.1, s32[6,32]{1,0:T(8,128)} %users_hbm.1, bf16[6,1024,128]{2,1,0:T(8,128)(2,1)} %pages_hbm.3), custom_call_target="tpu_custom_call" | custom-call | tf_op jit(solution)/shard_map/fetch/pallas_call | solution.py:198
  26.8 13.2 %match.1 = (f32[6,32]{1,0:T(8,128)}, bf16[64,32,128]{2,1,0:T(8,128)(2,1)}, bf16[6,1024,128]{2,1,0:T(8,128)(2,1)}) custom-call(s32[6,32]{1,0:T(8,128)} %get-tuple-element.10.place_ref, s32[6]{0:T(128)} %count_ref.1, f32[6,32]{1,0:T(8,128)} %teacher_ref.1, bf16[64,32,128]{2,1,0:T(8,128)(2,1)} %get-tuple-element.11.picked_hbm, bf16[6,1024,128]{2,1,0:T(8,128)(2,1)} %pages_hbm.3, ...), custom_call_target="tpu_custom_call" | custom-call | tf_op jit(solution)/shard_map/match/pallas_call | solution.py:476
  40.0 23.4 %give.1 = f32[1,32,128]{2,1,0:T(8,128)} custom-call(bf16[64,32,128]{2,1,0:T(8,128)(2,1)} %get-tuple-element.14.rows_hbm, s32[8,1,128]{2,1,0:T(1,128)} %get-tuple-element.15.info_ref), custom_call_target="tpu_custom_call" | custom-call | tf_op jit(solution)/shard_map/give/pallas_call | solution.py:593
  63.4 1.3 %copy.9 = f32[1,32,128]{2,1,0:T(8,128)} copy(f32[1,32,128]{2,1,0:T(8,128)} %give.1) | data formatting | bytes 32768

commit v4 on v3

--- a/solution.py
+++ b/solution.py
@@ -41,8 +41,8 @@
 
 
 def fetch_kernel(
-    query_hbm, users_hbm, pages_hbm, picked_hbm, place_ref, info_ref, page_t_hbm,
-    table, users_ref, pages_ref, page_t, asks_out, asks_in, asks_smem, chosen,
+    query_hbm, users_hbm, pages_hbm, picked_hbm, place_hbm, info_hbm, page_t_hbm,
+    table, users_ref, place_ref, pages_ref, page_t, asks_out, asks_in, asks_smem, chosen,
     z_send, y_send, q_recv, a_send, a_recv, c_send, c_recv, local_sem, in_sem, out_sem,
 ):
     me_g = lax.axis_index("group")
@@ -148,6 +148,8 @@
             preferred_element_type=jnp.float32,
         )
         place_ref[p : p + 1, :] = place[0:1].astype(jnp.int32)
+    place_out = pltpu.make_async_copy(place_ref, place_hbm, local_sem.at[2])
+    place_out.start()
     for p in range(n_pages):
         page_in(p).wait()
         page_t[p] = pages_ref[p].T
@@ -161,7 +163,8 @@
         ask_copy(k, (me_g + k) % GROUPS).wait_recv()
     to_smem = pltpu.make_async_copy(asks_in, asks_smem, local_sem.at[0])
     to_smem.start()
-    info_ref[...] = asks_in[...]
+    info_out = pltpu.make_async_copy(asks_in, info_hbm, local_sem.at[3])
+    info_out.start()
     to_smem.wait()
     for k in (0,) + Z_NEAR:
         for j in range(1, YS):
@@ -185,6 +188,8 @@
         for j in range(1, YS):
             y_copy(k, j, along(me_m, k, 0)).wait_send()
     own.wait()
+    place_out.wait()
+    info_out.wait()
     for k in range(1, GROUPS):
         chosen_copy(k, (me_g + k) % GROUPS).wait_recv()
         ask_copy(k, me_g).wait_send()
@@ -193,7 +198,6 @@
 
 def fetch(queries, users, pages):
     n_pages, n_tok, _ = pages.shape
-    vmem = pl.BlockSpec(memory_space=pltpu.VMEM)
     anywhere = pl.BlockSpec(memory_space=pl.ANY)
     return pl.pallas_call(
         fetch_kernel,
@@ -204,9 +208,10 @@
             jax.ShapeDtypeStruct((n_pages, DIM, n_tok), jnp.bfloat16),
         ),
         in_specs=[anywhere] * 3,
-        out_specs=[anywhere, vmem, vmem, anywhere],
+        out_specs=[anywhere] * 4,
         scratch_shapes=[
             pltpu.VMEM((MEMBERS, TOK, DIM), jnp.bfloat16),
+            pltpu.VMEM(users.shape, jnp.int32),
             pltpu.VMEM(users.shape, jnp.int32),
             pltpu.VMEM(pages.shape, jnp.bfloat16),
             pltpu.VMEM((n_pages, DIM, n_tok), jnp.bfloat16),
@@ -221,7 +226,7 @@
             pltpu.SemaphoreType.DMA((GROUPS,)),
             pltpu.SemaphoreType.DMA((GROUPS,)),
             pltpu.SemaphoreType.DMA((GROUPS,)),
-            pltpu.SemaphoreType.DMA((2,)),
+            pltpu.SemaphoreType.DMA((4,)),
             pltpu.SemaphoreType.DMA((n_pages,)),
             pltpu.SemaphoreType.DMA((n_pages,)),
         ],
@@ -242,10 +247,10 @@
 
 
 def match_kernel(
-    place_ref, count_ref, teacher_ref, picked_hbm, pages_hbm, page_t_hbm,
+    place_hbm, count_hbm, teacher_hbm, picked_hbm, pages_hbm, page_t_hbm,
     scores_ref, rows_ref, grad_hbm,
-    chunks, picked_ref, scaled, pages_ref, page_t, sims, logit, expo, stats, acc,
-    grad_ref, row_acc, score_l, same_slot, in_sem, out_sem,
+    chunks, place_ref, count_ref, teacher_ref, picked_ref, scaled, pages_ref, page_t, sims, logit, pending, stats, acc,
+    grad_ref, row_acc, score_l, same_slot, in_sem, out_sem, small_sem,
 ):
     n_pages, n_tok, _ = pages_ref.shape
     per_page = place_ref.shape[1] // CHUNK
@@ -257,35 +262,46 @@
 
     picked_in = pltpu.make_async_copy(picked_hbm, picked_ref, in_sem.at[n_pages])
     turned_in = pltpu.make_async_copy(page_t_hbm, page_t, in_sem.at[n_pages + 1])
+    smalls = [
+        pltpu.make_async_copy(source, dest, small_sem.at[i])
+        for i, (source, dest) in enumerate(
+            ((count_hbm, count_ref), (place_hbm, place_ref), (teacher_hbm, teacher_ref))
+        )
+    ]
+    for small in smalls:
+        small.start()
     picked_in.start()
     for p in range(n_pages):
         page_in(p).start()
     turned_in.start()
 
-    def list_chunk(n, total):
-        p = n // per_page
-        alive = (n % per_page) * CHUNK < count_ref[p]
-
-        @pl.when(alive)
-        def _():
-            chunks[total] = n
-
-        return total + alive.astype(jnp.int32)
-
-    total = lax.fori_loop(0, n_pages * per_page, list_chunk, 0)
-    for n in range(3):
-        chunks[total + n] = 0
-    pairs = (total + 1) // 2
     acc[...] = jnp.zeros_like(acc)
     row_acc[...] = jnp.zeros_like(row_acc)
     score_l[...] = jnp.zeros_like(score_l)
-    expo[...] = jnp.zeros_like(expo)
     logit[...] = jnp.zeros_like(logit)
     stats[...] = jnp.zeros_like(stats)
+    pending[...] = jnp.zeros_like(pending)
     seg_r = lax.broadcasted_iota(jnp.int32, (LANES, LANES), 0) >> 5
     seg_c = lax.broadcasted_iota(jnp.int32, (LANES, LANES), 1) >> 5
     same_slot[...] = jnp.where(seg_r == seg_c, 1.0, 0.0).astype(jnp.bfloat16)
     slot_of_lane = lax.broadcasted_iota(jnp.int32, (8, LANES), 1) >> 5
+    for small in smalls:
+        small.wait()
+
+    def list_chunk(n, total):
+        p = n // per_page
+        alive = (n % per_page) * CHUNK < count_ref[p]
+
+        @pl.when(alive)
+        def _():
+            chunks[total] = n
+
+        return total + alive.astype(jnp.int32)
+
+    total = lax.fori_loop(0, n_pages * per_page, list_chunk, jnp.int32(0))
+    for n in range(3):
+        chunks[total + n] = 0
+    pairs = (total + 1) // 2
     picked_in.wait()
 
     def scale_picked(n, carry):
@@ -345,21 +361,21 @@
             e = jnp.exp2(t)
             g = e * t
             logit[slot, at, :] = t
-            expo[slot, at, :] = e
             e, g = fold8(e, jnp.add), fold8(g, jnp.add)
             mass = e if mass is None else mass + e
             moment = g if moment is None else moment + g
         return mass, moment
 
-    def settle(n, slot):
+    def settle(n, slot, begun):
         p, c = where_of(n)
-        known = n < total
+        known = (n < total) & begun
         mass = jnp.broadcast_to(
             jnp.sum(stats[slot, MASS], axis=0, keepdims=True), (8, LANES)
         )
         moment = jnp.broadcast_to(
             jnp.sum(stats[slot, MOMENT], axis=0, keepdims=True), (8, LANES)
         )
+        mass = jnp.where(mass > 0.0, mass, 1.0)
         mean = moment / mass
         matched = (stats[slot, PEAK] + mean) * (1.0 / SCALE)
         score = split_dot(matched, same_slot[...])
@@ -381,7 +397,7 @@
             at = slice(start + 32 * i, start + 32 * i + 32)
             t = logit[slot, at, :]
             parts.append(
-                (expo[slot, at, :] * (tall(base, 32) + tall(slant, 32) * t)).astype(jnp.bfloat16)
+                (jnp.exp2(t) * (tall(base, 32) + tall(slant, 32) * t)).astype(jnp.bfloat16)
             )
         return jnp.concatenate(parts, axis=0)
 
@@ -390,8 +406,9 @@
         part = jnp.dot(page_t[p, :, at], slope, preferred_element_type=jnp.float32)
         return part if query_t is None else query_t + part
 
-    def add_rows(p, c, query_t):
-        query_part = query_t.T
+    def add_rows(n, slot):
+        p, c = where_of(n)
+        query_part = pending[slot].T
         for k in range(CHUNK):
             row_acc[place_ref[p, c * CHUNK + k]] += query_part[TOK * k : TOK * k + TOK]
 
@@ -404,7 +421,7 @@
             at = slice(quarter * b, quarter * b + quarter)
             slope = slope_rows(slot, base, slant, quarter * b, quarter)
             query_t = spread_rows(p, chosen, slope, at, query_t)
-        add_rows(p, c, query_t)
+        pending[slot] = query_t
 
     def turn(old, now, new, slot):
         p_old, c_old = where_of(old)
@@ -430,7 +447,7 @@
         stats[slot, TOP] = jnp.maximum(*tops)
         stats[slot, MASS] = mass
         stats[slot, MOMENT] = moment
-        add_rows(p_old, c_old, query_t)
+        pending[slot] = query_t
 
     similar(0, 0)
     similar(1, 1)
@@ -439,20 +456,30 @@
         n = 2 * i
         old = jnp.maximum(n - 2, 0)
 
+        settle(old + 1, 1, i > 0)
+        add_rows(jnp.maximum(n - 3, 0), 1)
         turn(old, n, n + 2, 0)
-        settle(n, 0)
+        settle(n, 0, True)
+        add_rows(old, 0)
         turn(old + 1, n + 1, n + 3, 1)
-        settle(n + 1, 1)
         return carry
 
     lax.fori_loop(0, pairs, step, 0)
-    spread(2 * pairs - 2, 0)
-    spread(2 * pairs - 1, 1)
 
     def page_out(p):
         return pltpu.make_async_copy(grad_ref.at[p], grad_hbm.at[p], out_sem.at[p])
 
-    for p in range(n_pages):
+    for p in range(n_pages - 2):
+        grad_ref[p] = acc[p].astype(jnp.bfloat16)
+        page_out(p).start()
+    last = 2 * pairs - 1
+    settle(last, 1, True)
+    add_rows(jnp.maximum(last - 2, 0), 1)
+    spread(last - 1, 0)
+    spread(last, 1)
+    add_rows(last - 1, 0)
+    add_rows(last, 1)
+    for p in range(n_pages - 2, n_pages):
         grad_ref[p] = acc[p].astype(jnp.bfloat16)
         page_out(p).start()
     col = lax.broadcasted_iota(jnp.int32, (LANES, 128), 1)
@@ -470,7 +497,6 @@
 def match(place, page_count, teacher, picked, pages, page_t):
     n_pages, n_tok, _ = pages.shape
     per_page = teacher.shape[1] // CHUNK
-    smem = pl.BlockSpec(memory_space=pltpu.SMEM)
     vmem = pl.BlockSpec(memory_space=pltpu.VMEM)
     anywhere = pl.BlockSpec(memory_space=pl.ANY)
     return pl.pallas_call(
@@ -480,17 +506,20 @@
             jax.ShapeDtypeStruct(picked.shape, jnp.bfloat16),
             jax.ShapeDtypeStruct(pages.shape, jnp.bfloat16),
         ),
-        in_specs=[smem, smem, smem, anywhere, anywhere, anywhere],
+        in_specs=[anywhere] * 6,
         out_specs=[vmem, vmem, anywhere],
         scratch_shapes=[
             pltpu.SMEM((n_pages * per_page + 3,), jnp.int32),
+            pltpu.SMEM(place.shape, jnp.int32),
+            pltpu.SMEM(page_count.shape, jnp.int32),
+            pltpu.SMEM(teacher.shape, jnp.float32),
             pltpu.VMEM(picked.shape, jnp.bfloat16),
             pltpu.VMEM((GROUPS * CAP, TOK, 2 * DIM), jnp.bfloat16),
             pltpu.VMEM(pages.shape, jnp.bfloat16),
             pltpu.VMEM((n_pages, DIM, n_tok), jnp.bfloat16),
             pltpu.VMEM((2, n_tok, LANES), jnp.float32),
             pltpu.VMEM((2, n_tok, LANES), jnp.float32),
-            pltpu.VMEM((2, n_tok, LANES), jnp.float32),
+            pltpu.VMEM((2, DIM, LANES), jnp.float32),
             pltpu.VMEM((2, 6, 8, LANES), jnp.float32),
             pltpu.VMEM((n_pages, n_tok, DIM), jnp.float32),
             pltpu.VMEM(pages.shape, jnp.bfloat16),
@@ -499,6 +528,7 @@
             pltpu.VMEM((LANES, LANES), jnp.bfloat16),
             pltpu.SemaphoreType.DMA((n_pages + 2,)),
             pltpu.SemaphoreType.DMA((n_pages,)),
+            pltpu.SemaphoreType.DMA((3,)),
         ],
         compiler_params=pltpu.CompilerParams(vmem_limit_bytes=60 * 1024 * 1024),
         name="match",
@@ -506,19 +536,22 @@
 
 
 def give_kernel(
-    rows_hbm, info_ref, out_ref,
-    rows_ref, landed, table, y_parts, z_sums, z_parts,
+    rows_hbm, info_hbm, out_ref,
+    rows_ref, info_ref, landed, table, y_parts, z_sums, z_parts,
     r_send, r_recv, y_send, y_recv, z_send, z_recv, local_sem,
 ):
     me_g = lax.axis_index("group")
     me_m = lax.axis_index("member")
     barrier, greeted = greet(me_g, me_m)
-    rows_in = pltpu.make_async_copy(rows_hbm, rows_ref, local_sem)
+    rows_in = pltpu.make_async_copy(rows_hbm, rows_ref, local_sem.at[0])
+    info_in = pltpu.make_async_copy(info_hbm, info_ref, local_sem.at[1])
     rows_in.start()
+    info_in.start()
     for s in range(GROUPS):
         for spare in range(CAP, 2 * CAP):
             landed[s, spare] = jnp.zeros((TOK, DIM), jnp.bfloat16)
     rows_in.wait()
+    info_in.wait()
     for n in range(CAP):
         landed[me_g, n] = rows_ref[me_g * CAP + n]
     pl.semaphore_wait(barrier, greeted)
@@ -595,11 +628,12 @@
         out_shape=jax.ShapeDtypeStruct((1, TOK, DIM), jnp.float32),
         in_specs=[
             pl.BlockSpec(memory_space=pl.ANY),
-            pl.BlockSpec(memory_space=pltpu.SMEM),
+            pl.BlockSpec(memory_space=pl.ANY),
         ],
         out_specs=pl.BlockSpec(memory_space=pltpu.VMEM),
         scratch_shapes=[
             pltpu.VMEM((GROUPS * CAP, TOK, DIM), jnp.bfloat16),
+            pltpu.SMEM(info.shape, jnp.int32),
             pltpu.VMEM((GROUPS, 2 * CAP, TOK, DIM), jnp.bfloat16),
             pltpu.VMEM((MEMBERS, TOK, DIM), jnp.bfloat16),
             pltpu.VMEM((MEMBERS, TOK, DIM), jnp.bfloat16),
@@ -611,7 +645,7 @@
             pltpu.SemaphoreType.DMA((MEMBERS,)),
             pltpu.SemaphoreType.DMA((ZS,)),
             pltpu.SemaphoreType.DMA((ZS,)),
-            pltpu.SemaphoreType.DMA,
+            pltpu.SemaphoreType.DMA((2,)),
         ],
         compiler_params=pltpu.CompilerParams(
             collective_id=1, has_side_effects=True, vmem_limit_bytes=60 * 1024 * 1024

time: 65.1 us -> 62.2 us (0.955)
  Pallas kernels: 62.8 us -> 59.6 us
    pallas_call x1, Pallas kernels: 23.4 us -> 21.9 us  [give(): pl.pallas_call(give_kernel, out_shape=jax.ShapeDtypeStruct((1, TOK, DIM),...]
    pallas_call x1, Pallas kernels: 13.2 us -> 12.1 us  [match(): pl.pallas_call(match_kernel, out_shape=(jax.ShapeDtypeStruct(teacher.shap...]
where the time goes in v4:
time: 62.2 us; the launch traced here: 61.6 us
  Pallas kernels  59.6 us (96%)
  local copies, waits for them, and re-layouts  1.32 us (2%)
  between operations  0.65 us (1%)
    pallas_call x1, Pallas kernels, fetch(): pl.pallas_call(fetch_kernel, out_shape=(jax.ShapeDtypeStruct((GROUPS * CA...  25.6 us
    pallas_call x1, Pallas kernels, give(): pl.pallas_call(give_kernel, out_shape=jax.ShapeDtypeStruct((1, TOK, DIM),...  21.9 us
    pallas_call x1, Pallas kernels, match(): pl.pallas_call(match_kernel, out_shape=(jax.ShapeDtypeStruct(teacher.shap...  12.1 us
    unnamed x1, local copies, waits for them, and re-layouts  1.32 us

profile of v4, /device:TPU:1, one launch (start us, length us, event | category | flops | bytes accessed | tf_op | source)
XLA Modules:
  0.0 61.6 jit_solution(12045359111152900183)
XLA Ops:
  0.6 25.6 %fetch.1 = (bf16[64,32,128]{2,1,0:T(8,128)(2,1)}, s32[6,32]{1,0:T(8,128)}, s32[8,1,128]{2,1,0:T(1,128)}, bf16[6,128,1024]{2,1,0:T(8,128)(2,1)}) custom-call(bf16[1,32,128]{2,1,0:T(8,128)(2,1)} %query_hbm.1, s32[6,32]{1,0:T(8,128)} %users_hbm.1, bf16[6,1024,128]{2,1,0:T(8,128)(2,1)} %pages_hbm.3), custom_call_target="tpu_custom_call" | custom-call | tf_op jit(solution)/shard_map/fetch/pallas_call | solution.py:202
  26.3 12.1 %match.1 = (f32[6,32]{1,0:T(8,128)}, bf16[64,32,128]{2,1,0:T(8,128)(2,1)}, bf16[6,1024,128]{2,1,0:T(8,128)(2,1)}) custom-call(s32[6,32]{1,0:T(8,128)} %get-tuple-element.10.place_hbm, s32[6]{0:T(128)} %count_hbm.1, f32[6,32]{1,0:T(8,128)} %teacher_hbm.1, bf16[64,32,128]{2,1,0:T(8,128)(2,1)} %get-tuple-element.11.picked_hbm, bf16[6,1024,128]{2,1,0:T(8,128)(2,1)} %pages_hbm.3, ...), custom_call_target="tpu_custom_call" | custom-call | tf_op jit(solution)/shard_map/match/pallas_call | solution.py:502
  38.4 21.9 %give.1 = f32[1,32,128]{2,1,0:T(8,128)} custom-call(bf16[64,32,128]{2,1,0:T(8,128)(2,1)} %get-tuple-element.14.rows_hbm, s32[8,1,128]{2,1,0:T(1,128)} %get-tuple-element.15.info_hbm), custom_call_target="tpu_custom_call" | custom-call | tf_op jit(solution)/shard_map/give/pallas_call | solution.py:626
  60.3 1.3 %copy.9 = f32[1,32,128]{2,1,0:T(8,128)} copy(f32[1,32,128]{2,1,0:T(8,128)} %give.1) | data formatting | bytes 32768

commit v5 on v4

--- a/solution.py
+++ b/solution.py
@@ -13,6 +13,7 @@
 GROUPS = 8
 MEMBERS = 32
 TOK = 32
+HALF = TOK // 2
 ZS, YS = 8, 4
 Z_FAR = (4, 3, 5, 2, 6, 1, 7)
 Z_NEAR = (1, 7, 2, 6, 3, 5, 4)
@@ -248,9 +249,9 @@
 
 def match_kernel(
     place_hbm, count_hbm, teacher_hbm, picked_hbm, pages_hbm, page_t_hbm,
-    scores_ref, rows_ref, grad_hbm,
+    scores_hbm, rows_hbm, grad_hbm,
     chunks, place_ref, count_ref, teacher_ref, picked_ref, scaled, pages_ref, page_t, sims, logit, pending, stats, acc,
-    grad_ref, row_acc, score_l, same_slot, in_sem, out_sem, small_sem,
+    grad_ref, row_acc, score_l, same_slot, scores_ref, rows_ref, in_sem, out_sem, small_sem,
 ):
     n_pages, n_tok, _ = pages_ref.shape
     per_page = place_ref.shape[1] // CHUNK
@@ -312,9 +313,8 @@
         return carry
 
     lax.fori_loop(0, picked_ref.shape[0], scale_picked, 0, unroll=8)
-    for p in range(n_pages):
+    for p in range(2):
         page_in(p).wait()
-    turned_in.wait()
 
     def where_of(n):
         code = chunks[n]
@@ -451,6 +451,9 @@
 
     similar(0, 0)
     similar(1, 1)
+    for p in range(2, n_pages):
+        page_in(p).wait()
+    turned_in.wait()
 
     def step(i, carry):
         n = 2 * i
@@ -477,11 +480,14 @@
     add_rows(jnp.maximum(last - 2, 0), 1)
     spread(last - 1, 0)
     spread(last, 1)
-    add_rows(last - 1, 0)
-    add_rows(last, 1)
     for p in range(n_pages - 2, n_pages):
         grad_ref[p] = acc[p].astype(jnp.bfloat16)
         page_out(p).start()
+    add_rows(last - 1, 0)
+    add_rows(last, 1)
+    rows_ref[...] = row_acc[...].astype(jnp.bfloat16)
+    rows_out = pltpu.make_async_copy(rows_ref, rows_hbm, small_sem.at[0])
+    rows_out.start()
     col = lax.broadcasted_iota(jnp.int32, (LANES, 128), 1)
     row = lax.broadcasted_iota(jnp.int32, (LANES, 128), 0)
     out = jnp.zeros((8, 128), jnp.float32)
@@ -489,7 +495,10 @@
         take = jnp.where(row == (col - c * CHUNK) * TOK, 1.0, 0.0)
         out += split_dot(score_l[c], take.astype(jnp.bfloat16))
     scores_ref[...] = out[: scores_ref.shape[0], : scores_ref.shape[1]]
-    rows_ref[...] = row_acc[...].astype(jnp.bfloat16)
+    scores_out = pltpu.make_async_copy(scores_ref, scores_hbm, small_sem.at[1])
+    scores_out.start()
+    rows_out.wait()
+    scores_out.wait()
     for p in range(n_pages):
         page_out(p).wait()
 
@@ -497,7 +506,6 @@
 def match(place, page_count, teacher, picked, pages, page_t):
     n_pages, n_tok, _ = pages.shape
     per_page = teacher.shape[1] // CHUNK
-    vmem = pl.BlockSpec(memory_space=pltpu.VMEM)
     anywhere = pl.BlockSpec(memory_space=pl.ANY)
     return pl.pallas_call(
         match_kernel,
@@ -507,7 +515,7 @@
             jax.ShapeDtypeStruct(pages.shape, jnp.bfloat16),
         ),
         in_specs=[anywhere] * 6,
-        out_specs=[vmem, vmem, anywhere],
+        out_specs=[anywhere] * 3,
         scratch_shapes=[
             pltpu.SMEM((n_pages * per_page + 3,), jnp.int32),
             pltpu.SMEM(place.shape, jnp.int32),
@@ -526,6 +534,8 @@
             pltpu.VMEM(picked.shape, jnp.float32),
             pltpu.VMEM((per_page, 8, LANES), jnp.float32),
             pltpu.VMEM((LANES, LANES), jnp.bfloat16),
+            pltpu.VMEM(teacher.shape, jnp.float32),
+            pltpu.VMEM(picked.shape, jnp.bfloat16),
             pltpu.SemaphoreType.DMA((n_pages + 2,)),
             pltpu.SemaphoreType.DMA((n_pages,)),
             pltpu.SemaphoreType.DMA((3,)),
@@ -537,7 +547,7 @@
 
 def give_kernel(
     rows_hbm, info_hbm, out_ref,
-    rows_ref, info_ref, landed, table, y_parts, z_sums, z_parts,
+    rows_ref, info_ref, landed_a, landed_b, table, y_parts, z_sums, z_parts,
     r_send, r_recv, y_send, y_recv, z_send, z_recv, local_sem,
 ):
     me_g = lax.axis_index("group")
@@ -547,13 +557,16 @@
     info_in = pltpu.make_async_copy(info_hbm, info_ref, local_sem.at[1])
     rows_in.start()
     info_in.start()
+    landed = (landed_a, landed_b)
     for s in range(GROUPS):
         for spare in range(CAP, 2 * CAP):
-            landed[s, spare] = jnp.zeros((TOK, DIM), jnp.bfloat16)
+            for h in range(2):
+                landed[h][s, spare] = jnp.zeros((HALF, DIM), jnp.bfloat16)
     rows_in.wait()
     info_in.wait()
     for n in range(CAP):
-        landed[me_g, n] = rows_ref[me_g * CAP + n]
+        for h in range(2):
+            landed[h][me_g, n] = rows_ref[me_g * CAP + n, HALF * h : HALF * h + HALF]
     pl.semaphore_wait(barrier, greeted)
 
     def remote(src, dst, send, recv, g, m):
@@ -562,64 +575,73 @@
             device_id=(g, m), device_id_type=MESH,
         )
 
-    def row_copy(k, src_g):
+    def row_copy(h, k, src_g):
         peer = (me_g + k) % GROUPS
         return remote(
-            rows_ref.at[pl.ds(peer * CAP, CAP)], landed.at[src_g, pl.ds(0, CAP)],
-            r_send.at[k], r_recv.at[src_g], peer, me_m,
-        )
-
-    def y_copy(k, j, slot):
+            rows_ref.at[pl.ds(peer * CAP, CAP), pl.ds(HALF * h, HALF)],
+            landed[h].at[src_g, pl.ds(0, CAP)],
+            r_send.at[h, k], r_recv.at[h, src_g], peer, me_m,
+        )
+
+    def y_copy(h, k, j, slot):
         return remote(
-            table.at[YS * k + j], y_parts.at[YS * k + slot],
-            y_send.at[YS * k + j], y_recv.at[YS * k + slot], me_g, along(me_m, 0, j),
-        )
-
-    def z_copy(k, slot):
+            table.at[h, YS * k + j], y_parts.at[h, YS * k + slot],
+            y_send.at[h, YS * k + j], y_recv.at[h, YS * k + slot], me_g, along(me_m, 0, j),
+        )
+
+    def z_copy(h, k, slot):
         return remote(
-            z_sums.at[k], z_parts.at[slot], z_send.at[k], z_recv.at[slot],
+            z_sums.at[h, k], z_parts.at[h, slot], z_send.at[h, k], z_recv.at[h, slot],
             me_g, along(me_m, k, 0),
         )
 
-    for k in (4, 5, 2, 3, 6, 7, 1):
-        row_copy(k, me_g).start()
-    for k in range(1, GROUPS):
-        row_copy(k, (me_g + k) % GROUPS).wait_recv()
-
-    def total_of(owner):
-        total = jnp.zeros((TOK, DIM), jnp.float32)
+    def total_of(h, owner):
+        total = jnp.zeros((HALF, DIM), jnp.float32)
         for s in range(GROUPS):
-            total += landed[s, info_ref[s, 0, INV_AT + owner] & (2 * CAP - 1)].astype(
+            total += landed[h][s, info_ref[s, 0, INV_AT + owner] & (2 * CAP - 1)].astype(
                 jnp.float32
             )
         return total
 
-    for k in Z_FAR + (0,):
-        for j in Y_FAR:
-            table[YS * k + j] = total_of(along(me_m, k, j)).astype(jnp.bfloat16)
-            y_copy(k, j, YS - j).start()
-    mine = None
-    for k in Z_FAR + (0,):
-        total = total_of(along(me_m, k, 0))
-        for j in (1, 3, 2):
-            y_copy(k, j, j).wait_recv()
-            total += y_parts[YS * k + j].astype(jnp.float32)
-        if k:
-            z_sums[k] = total.astype(jnp.bfloat16)
-            z_copy(k, ZS - k).start()
-        else:
-            mine = total
-    for k in Z_NEAR:
-        z_copy(k, k).wait_recv()
-        mine += z_parts[k].astype(jnp.float32)
-    out_ref[0] = mine
-    for k in range(1, GROUPS):
-        row_copy(k, me_g).wait_send()
-    for k in range(ZS):
-        for j in range(1, YS):
-            y_copy(k, j, j).wait_send()
-        if k:
-            z_copy(k, k).wait_send()
+    mine = [None, None]
+
+    def sum_y(h):
+        for k in Z_FAR + (0,):
+            total = total_of(h, along(me_m, k, 0))
+            for j in (1, 3, 2):
+                y_copy(h, k, j, j).wait_recv()
+                total += y_parts[h, YS * k + j].astype(jnp.float32)
+            if k:
+                z_sums[h, k] = total.astype(jnp.bfloat16)
+                z_copy(h, k, ZS - k).start()
+            else:
+                mine[h] = total
+
+    for h in range(2):
+        for k in (4, 5, 2, 3, 6, 7, 1):
+            row_copy(h, k, me_g).start()
+    for h in range(2):
+        for k in range(1, GROUPS):
+            row_copy(h, k, (me_g + k) % GROUPS).wait_recv()
+        for k in Z_FAR + (0,):
+            for j in Y_FAR:
+                table[h, YS * k + j] = total_of(h, along(me_m, k, j)).astype(jnp.bfloat16)
+                y_copy(h, k, j, YS - j).start()
+    for h in range(2):
+        sum_y(h)
+    for h in range(2):
+        for k in Z_NEAR:
+            z_copy(h, k, k).wait_recv()
+            mine[h] += z_parts[h, k].astype(jnp.float32)
+        out_ref[0, HALF * h : HALF * h + HALF] = mine[h]
+    for h in range(2):
+        for k in range(1, GROUPS):
+            row_copy(h, k, me_g).wait_send()
+        for k in range(ZS):
+            for j in range(1, YS):
+                y_copy(h, k, j, j).wait_send()
+            if k:
+                z_copy(h, k, k).wait_send()
 
 
 def give(rows, info):
@@ -634,17 +656,18 @@
         scratch_shapes=[
             pltpu.VMEM((GROUPS * CAP, TOK, DIM), jnp.bfloat16),
             pltpu.SMEM(info.shape, jnp.int32),
-            pltpu.VMEM((GROUPS, 2 * CAP, TOK, DIM), jnp.bfloat16),
-            pltpu.VMEM((MEMBERS, TOK, DIM), jnp.bfloat16),
-            pltpu.VMEM((MEMBERS, TOK, DIM), jnp.bfloat16),
-            pltpu.VMEM((ZS, TOK, DIM), jnp.bfloat16),
-            pltpu.VMEM((ZS, TOK, DIM), jnp.bfloat16),
-            pltpu.SemaphoreType.DMA((GROUPS,)),
-            pltpu.SemaphoreType.DMA((GROUPS,)),
-            pltpu.SemaphoreType.DMA((MEMBERS,)),
-            pltpu.SemaphoreType.DMA((MEMBERS,)),
-            pltpu.SemaphoreType.DMA((ZS,)),
-            pltpu.SemaphoreType.DMA((ZS,)),
+            pltpu.VMEM((GROUPS, 2 * CAP, HALF, DIM), jnp.bfloat16),
+            pltpu.VMEM((GROUPS, 2 * CAP, HALF, DIM), jnp.bfloat16),
+            pltpu.VMEM((2, MEMBERS, HALF, DIM), jnp.bfloat16),
+            pltpu.VMEM((2, MEMBERS, HALF, DIM), jnp.bfloat16),
+            pltpu.VMEM((2, ZS, HALF, DIM), jnp.bfloat16),
+            pltpu.VMEM((2, ZS, HALF, DIM), jnp.bfloat16),
+            pltpu.SemaphoreType.DMA((2, GROUPS)),
+            pltpu.SemaphoreType.DMA((2, GROUPS)),
+            pltpu.SemaphoreType.DMA((2, MEMBERS)),
+            pltpu.SemaphoreType.DMA((2, MEMBERS)),
+            pltpu.SemaphoreType.DMA((2, ZS)),
+            pltpu.SemaphoreType.DMA((2, ZS)),
             pltpu.SemaphoreType.DMA((2,)),
         ],
         compiler_params=pltpu.CompilerParams(

time: 62.2 us -> 61.8 us (level)
    pallas_call x1, Pallas kernels: 21.9 us -> 22.9 us  [give(): pl.pallas_call(give_kernel, out_shape=jax.ShapeDtypeStruct((1, TOK, DIM),...]
    pallas_call x1, Pallas kernels: 12.1 us -> 11.1 us  [match(): pl.pallas_call(match_kernel, out_shape=(jax.ShapeDtypeStruct(teacher.shap...]
where the time goes in v5:
time: 61.8 us; the launch traced here: 61.6 us
  Pallas kernels  59.6 us (96%)
  local copies, waits for them, and re-layouts  1.32 us (2%)
  between operations  0.65 us (1%)
    pallas_call x1, Pallas kernels, fetch(): pl.pallas_call(fetch_kernel, out_shape=(jax.ShapeDtypeStruct((GROUPS * CA...  25.6 us
    pallas_call x1, Pallas kernels, give(): pl.pallas_call(give_kernel, out_shape=jax.ShapeDtypeStruct((1, TOK, DIM),...  22.9 us
    pallas_call x1, Pallas kernels, match(): pl.pallas_call(match_kernel, out_shape=(jax.ShapeDtypeStruct(teacher.shap...  11.1 us
    unnamed x1, local copies, waits for them, and re-layouts  1.32 us

profile of v5, /device:TPU:1, one launch (start us, length us, event | category | flops | bytes accessed | tf_op | source)
XLA Modules:
  0.0 61.6 jit_solution(13209923850364481726)
XLA Ops:
  0.6 25.6 %fetch.1 = (bf16[64,32,128]{2,1,0:T(8,128)(2,1)}, s32[6,32]{1,0:T(8,128)}, s32[8,1,128]{2,1,0:T(1,128)}, bf16[6,128,1024]{2,1,0:T(8,128)(2,1)}) custom-call(bf16[1,32,128]{2,1,0:T(8,128)(2,1)} %query_hbm.1, s32[6,32]{1,0:T(8,128)} %users_hbm.1, bf16[6,1024,128]{2,1,0:T(8,128)(2,1)} %pages_hbm.3), custom_call_target="tpu_custom_call" | custom-call | tf_op jit(solution)/shard_map/fetch/pallas_call | solution.py:203
  26.3 11.1 %match.1 = (f32[6,32]{1,0:T(8,128)}, bf16[64,32,128]{2,1,0:T(8,128)(2,1)}, bf16[6,1024,128]{2,1,0:T(8,128)(2,1)}) custom-call(s32[6,32]{1,0:T(8,128)} %get-tuple-element.10.place_hbm, s32[6]{0:T(128)} %count_hbm.1, f32[6,32]{1,0:T(8,128)} %teacher_hbm.1, bf16[64,32,128]{2,1,0:T(8,128)(2,1)} %get-tuple-element.11.picked_hbm, bf16[6,1024,128]{2,1,0:T(8,128)(2,1)} %pages_hbm.3, ...), custom_call_target="tpu_custom_call" | custom-call | tf_op jit(solution)/shard_map/match/pallas_call | solution.py:510
  37.4 22.9 %give.1 = f32[1,32,128]{2,1,0:T(8,128)} custom-call(bf16[64,32,128]{2,1,0:T(8,128)(2,1)} %get-tuple-element.14.rows_hbm, s32[8,1,128]{2,1,0:T(1,128)} %get-tuple-element.15.info_hbm), custom_call_target="tpu_custom_call" | custom-call | tf_op jit(solution)/shard_map/give/pallas_call | solution.py:648
  60.3 1.3 %copy.9 = f32[1,32,128]{2,1,0:T(8,128)} copy(f32[1,32,128]{2,1,0:T(8,128)} %give.1) | data formatting | bytes 32768

commit v6 on v5

--- a/solution.py
+++ b/solution.py
@@ -43,7 +43,8 @@
 
 def fetch_kernel(
     query_hbm, users_hbm, pages_hbm, picked_hbm, place_hbm, info_hbm, page_t_hbm,
-    table, users_ref, place_ref, pages_ref, page_t, asks_out, asks_in, asks_smem, chosen,
+    table_a, table_b, users_ref, place_ref, pages_ref, page_t, asks_out, asks_in, asks_smem,
+    chosen,
     z_send, y_send, q_recv, a_send, a_recv, c_send, c_recv, local_sem, in_sem, out_sem,
 ):
     me_g = lax.axis_index("group")
@@ -51,9 +52,16 @@
     n_pages = pages_hbm.shape[0]
     barrier, greeted = greet(me_g, me_m)
     users_in = pltpu.make_async_copy(users_hbm, users_ref, local_sem.at[0])
-    query_in = pltpu.make_async_copy(query_hbm.at[0], table.at[me_m], local_sem.at[1])
+    table = (table_a, table_b)
+    queries_in = [
+        pltpu.make_async_copy(
+            query_hbm.at[0, pl.ds(HALF * h, HALF)], table[h].at[me_m], local_sem.at[1 + 3 * h]
+        )
+        for h in range(2)
+    ]
     users_in.start()
-    query_in.start()
+    for query_in in queries_in:
+        query_in.start()
 
     def page_in(p):
         return pltpu.make_async_copy(pages_hbm.at[p], pages_ref.at[p], in_sem.at[p])
@@ -101,7 +109,8 @@
     asks = (ids + spread).astype(jnp.int32)
     for g in range(GROUPS):
         asks_out[g] = asks[g : g + 1, :]
-    query_in.wait()
+    for query_in in queries_in:
+        query_in.wait()
 
     def remote(src, dst, send, recv, g, m):
         return pltpu.make_async_remote_copy(
@@ -109,16 +118,16 @@
             device_id=(g, m), device_id_type=MESH,
         )
 
-    def z_copy(k, src_m):
+    def z_copy(h, k, src_m):
         return remote(
-            table.at[src_m], table.at[src_m], z_send.at[k], q_recv.at[src_m],
+            table[h].at[src_m], table[h].at[src_m], z_send.at[h, k], q_recv.at[h, src_m],
             me_g, along(me_m, k, 0),
         )
 
-    def y_copy(k, j, src_m):
+    def y_copy(h, k, j, src_m):
         return remote(
-            table.at[src_m], table.at[src_m], y_send.at[YS * k + j], q_recv.at[src_m],
-            me_g, along(me_m, 0, j),
+            table[h].at[src_m], table[h].at[src_m],
+            y_send.at[h, YS * k + j], q_recv.at[h, src_m], me_g, along(me_m, 0, j),
         )
 
     def ask_copy(k, src_g):
@@ -127,20 +136,21 @@
             asks_out.at[peer], asks_in.at[src_g], a_send.at[k], a_recv.at[src_g], peer, me_m
         )
 
-    def chosen_copy(k, src_g):
+    def chosen_copy(h, k, src_g):
         peer = (me_g + k) % GROUPS
         return remote(
-            chosen.at[k], picked_hbm.at[pl.ds(src_g * CAP, CAP)],
-            c_send.at[k], c_recv.at[src_g], peer, me_m,
+            chosen.at[h, k], picked_hbm.at[pl.ds(src_g * CAP, CAP), pl.ds(HALF * h, HALF)],
+            c_send.at[h, k], c_recv.at[h, src_g], peer, me_m,
         )
 
     pl.semaphore_wait(barrier, greeted)
-    for k in Z_FAR:
-        z_copy(k, me_m).start()
-    for j in Y_FAR:
-        y_copy(0, j, me_m).start()
     for k in range(1, GROUPS):
         ask_copy(k, me_g).start()
+    for h in range(2):
+        for k in Z_FAR:
+            z_copy(h, k, me_m).start()
+        for j in Y_FAR:
+            y_copy(h, 0, j, me_m).start()
     asks_in[me_g] = asks_out[me_g]
     spot = ((lane8 >> 5) * CAP).astype(jnp.float32) + rank
     for p in range(rows):
@@ -155,11 +165,12 @@
         page_in(p).wait()
         page_t[p] = pages_ref[p].T
         page_out(p).start()
-    for k in Z_NEAR:
-        src = along(me_m, k, 0)
-        z_copy(k, src).wait_recv()
-        for j in Y_FAR:
-            y_copy(k, j, src).start()
+    for h in range(2):
+        for k in Z_NEAR:
+            src = along(me_m, k, 0)
+            z_copy(h, k, src).wait_recv()
+            for j in Y_FAR:
+                y_copy(h, k, j, src).start()
     for k in range(1, GROUPS):
         ask_copy(k, (me_g + k) % GROUPS).wait_recv()
     to_smem = pltpu.make_async_copy(asks_in, asks_smem, local_sem.at[0])
@@ -167,34 +178,40 @@
     info_out = pltpu.make_async_copy(asks_in, info_hbm, local_sem.at[3])
     info_out.start()
     to_smem.wait()
-    for k in (0,) + Z_NEAR:
-        for j in range(1, YS):
-            y_copy(k, j, along(me_m, k, j)).wait_recv()
-
-    for k in (4, 5, 2, 3, 6, 7, 1, 0):
-        peer = (me_g + k) % GROUPS
-        for n in range(CAP):
-            chosen[k, n] = table[asks_smem[peer, 0, n] & (MEMBERS - 1)]
-        if k:
-            chosen_copy(k, me_g).start()
-    own = pltpu.make_async_copy(
-        chosen.at[0], picked_hbm.at[pl.ds(me_g * CAP, CAP)], local_sem.at[1]
-    )
-    own.start()
+    owns = []
+    for h in range(2):
+        for k in (0,) + Z_NEAR:
+            for j in range(1, YS):
+                y_copy(h, k, j, along(me_m, k, j)).wait_recv()
+        for k in (4, 5, 2, 3, 6, 7, 1, 0):
+            peer = (me_g + k) % GROUPS
+            for n in range(CAP):
+                chosen[h, k, n] = table[h][asks_smem[peer, 0, n] & (MEMBERS - 1)]
+            if k:
+                chosen_copy(h, k, me_g).start()
+        own = pltpu.make_async_copy(
+            chosen.at[h, 0],
+            picked_hbm.at[pl.ds(me_g * CAP, CAP), pl.ds(HALF * h, HALF)],
+            local_sem.at[1 + 3 * h],
+        )
+        own.start()
+        owns.append(own)
     for p in range(n_pages):
         page_out(p).wait()
-    for k in Z_NEAR:
-        z_copy(k, me_m).wait_send()
-    for k in (0,) + Z_NEAR:
-        for j in range(1, YS):
-            y_copy(k, j, along(me_m, k, 0)).wait_send()
-    own.wait()
+    for h in range(2):
+        for k in Z_NEAR:
+            z_copy(h, k, me_m).wait_send()
+        for k in (0,) + Z_NEAR:
+            for j in range(1, YS):
+                y_copy(h, k, j, along(me_m, k, 0)).wait_send()
+        owns[h].wait()
     place_out.wait()
     info_out.wait()
     for k in range(1, GROUPS):
-        chosen_copy(k, (me_g + k) % GROUPS).wait_recv()
         ask_copy(k, me_g).wait_send()
-        chosen_copy(k, me_g).wait_send()
+        for h in range(2):
+            chosen_copy(h, k, (me_g + k) % GROUPS).wait_recv()
+            chosen_copy(h, k, me_g).wait_send()
 
 
 def fetch(queries, users, pages):
@@ -211,7 +228,8 @@
         in_specs=[anywhere] * 3,
         out_specs=[anywhere] * 4,
         scratch_shapes=[
-            pltpu.VMEM((MEMBERS, TOK, DIM), jnp.bfloat16),
+            pltpu.VMEM((MEMBERS, HALF, DIM), jnp.bfloat16),
+            pltpu.VMEM((MEMBERS, HALF, DIM), jnp.bfloat16),
             pltpu.VMEM(users.shape, jnp.int32),
             pltpu.VMEM(users.shape, jnp.int32),
             pltpu.VMEM(pages.shape, jnp.bfloat16),
@@ -219,15 +237,15 @@
             pltpu.VMEM((GROUPS, 1, 128), jnp.int32),
             pltpu.VMEM((GROUPS, 1, 128), jnp.int32),
             pltpu.SMEM((GROUPS, 1, 128), jnp.int32),
-            pltpu.VMEM((GROUPS, CAP, TOK, DIM), jnp.bfloat16),
-            pltpu.SemaphoreType.DMA((ZS,)),
-            pltpu.SemaphoreType.DMA((MEMBERS,)),
-            pltpu.SemaphoreType.DMA((MEMBERS,)),
+            pltpu.VMEM((2, GROUPS, CAP, HALF, DIM), jnp.bfloat16),
+            pltpu.SemaphoreType.DMA((2, ZS)),
+            pltpu.SemaphoreType.DMA((2, MEMBERS)),
+            pltpu.SemaphoreType.DMA((2, MEMBERS)),
             pltpu.SemaphoreType.DMA((GROUPS,)),
             pltpu.SemaphoreType.DMA((GROUPS,)),
-            pltpu.SemaphoreType.DMA((GROUPS,)),
-            pltpu.SemaphoreType.DMA((GROUPS,)),
-            pltpu.SemaphoreType.DMA((4,)),
+            pltpu.SemaphoreType.DMA((2, GROUPS)),
+            pltpu.SemaphoreType.DMA((2, GROUPS)),
+            pltpu.SemaphoreType.DMA((5,)),
             pltpu.SemaphoreType.DMA((n_pages,)),
             pltpu.SemaphoreType.DMA((n_pages,)),
         ],

time: 61.8 us -> 62.4 us (level)
  Pallas kernels: 59.6 us -> 60.3 us
where the time goes in v6:
time: 62.4 us; the launch traced here: 62.2 us
  Pallas kernels  60.3 us (97%)
  local copies, waits for them, and re-layouts  1.32 us (2%)
  between operations  0.65 us (1%)
    pallas_call x1, Pallas kernels, fetch(): pl.pallas_call(fetch_kernel, out_shape=(jax.ShapeDtypeStruct((GROUPS * CA...  26.2 us
    pallas_call x1, Pallas kernels, give(): pl.pallas_call(give_kernel, out_shape=jax.ShapeDtypeStruct((1, TOK, DIM),...  23 us
    pallas_call x1, Pallas kernels, match(): pl.pallas_call(match_kernel, out_shape=(jax.ShapeDtypeStruct(teacher.shap...  11.1 us
    unnamed x1, local copies, waits for them, and re-layouts  1.32 us

profile of v6, /device:TPU:1, one launch (start us, length us, event | category | flops | bytes accessed | tf_op | source)
XLA Modules:
  0.0 62.2 jit_solution(13336710772287250459)
XLA Ops:
  0.6 26.2 %fetch.1 = (bf16[64,32,128]{2,1,0:T(8,128)(2,1)}, s32[6,32]{1,0:T(8,128)}, s32[8,1,128]{2,1,0:T(1,128)}, bf16[6,128,1024]{2,1,0:T(8,128)(2,1)}) custom-call(bf16[1,32,128]{2,1,0:T(8,128)(2,1)} %query_hbm.1, s32[6,32]{1,0:T(8,128)} %users_hbm.1, bf16[6,1024,128]{2,1,0:T(8,128)(2,1)} %pages_hbm.3), custom_call_target="tpu_custom_call" | custom-call | tf_op jit(solution)/shard_map/fetch/pallas_call | solution.py:220
  26.8 11.1 %match.1 = (f32[6,32]{1,0:T(8,128)}, bf16[64,32,128]{2,1,0:T(8,128)(2,1)}, bf16[6,1024,128]{2,1,0:T(8,128)(2,1)}) custom-call(s32[6,32]{1,0:T(8,128)} %get-tuple-element.10.place_hbm, s32[6]{0:T(128)} %count_hbm.1, f32[6,32]{1,0:T(8,128)} %teacher_hbm.1, bf16[64,32,128]{2,1,0:T(8,128)(2,1)} %get-tuple-element.11.picked_hbm, bf16[6,1024,128]{2,1,0:T(8,128)(2,1)} %pages_hbm.3, ...), custom_call_target="tpu_custom_call" | custom-call | tf_op jit(solution)/shard_map/match/pallas_call | solution.py:528
  37.9 23.0 %give.1 = f32[1,32,128]{2,1,0:T(8,128)} custom-call(bf16[64,32,128]{2,1,0:T(8,128)(2,1)} %get-tuple-element.14.rows_hbm, s32[8,1,128]{2,1,0:T(1,128)} %get-tuple-element.15.info_hbm), custom_call_target="tpu_custom_call" | custom-call | tf_op jit(solution)/shard_map/give/pallas_call | solution.py:666
  60.9 1.3 %copy.9 = f32[1,32,128]{2,1,0:T(8,128)} copy(f32[1,32,128]{2,1,0:T(8,128)} %give.1) | data formatting | bytes 32768
